TPU v7x, 128 devices: a whole 4x4x4 slice. The times are simulated.
128 devices in a mesh: ctx: 32 (over y, x, core), head: 4 (over z).
Axes of the slice: x: 4, y: 4, z: 4, core: 2. Of those that a mesh axis runs over, the one named last changes fastest.
Arguments:
- tokens: bfloat16 [8192, 3072], P('ctx', 'head'), may hold values from -6 to 6
- w_qkv: bfloat16 [3, 3072, 3072], P(None, None, 'head'), may hold values from -0.109375 to 0.109375
- w_out: bfloat16 [3072, 3072], P('head'), may hold values from -2 to 2
- block_perm: int32 [128], replicated, may hold values from 0 to 127, as said below
Outputs:
- mixed: bfloat16 [8192, 3072], P('ctx', 'head')
Inputs may be any that keep to these rules, and one draw needn't show every extreme that they name: A permutation; slot s holds frame row block_perm[s], token rows s * 64 to (s + 1) * 64 - 1 of tokens. Cut the frame rows into 64 runs of 2 consecutive rows, numbered 0 up; each index of ctx holds, for one c of its own, run c in its first 2 slots and run 2 * 32 - 1 - c in its last 2 slots, in row order.
All inputs are finite; a program needn't handle non-finite values.
Results may differ from a plain program's by a relative error of at most 0.02.
Values may be sent and summed in bfloat16 or wider, within the bound.
A program may use at most 192 MiB of HBM per device.

v0:
```python
import jax
import jax.numpy as jnp
from jax import lax
from jax.sharding import PartitionSpec as P

HD = 128
WW = 64
F = 8


ROPE_BASE = 10000.0
EPSILON = 1e-06


def from_everyone(shard, axis):
    count = lax.axis_size(axis)
    return lax.all_to_all(
        jnp.broadcast_to(shard[None], (count, *shard.shape)), axis, 0, 0, tiled=True
    )


def laid_out(parts, dim):
    parts = jnp.moveaxis(parts, 0, dim)
    lengths = parts.shape
    return parts.reshape(*lengths[:dim], lengths[dim] * lengths[dim + 1], *lengths[dim + 2 :])


def gather_directly(shard, axis, dim):
    parts = from_everyone(shard, axis)
    return laid_out(parts, dim)


def cut_along(shard, dim, count):
    lengths = shard.shape
    parts = shard.reshape(*lengths[:dim], count, lengths[dim] // count, *lengths[dim + 1 :])
    return jnp.moveaxis(parts, dim, 0)


def sum_at_owner(shard, axis, dim):
    parts = cut_along(shard, dim, lax.axis_size(axis))
    arrived = lax.all_to_all(parts, axis, split_axis=0, concat_axis=0, tiled=True)
    return arrived.astype(jnp.float32).sum(axis=0)


def frames_and_rows(block_perm, frame_total):
    frame_rows = block_perm.shape[0] // frame_total
    slot_frame = block_perm // frame_rows
    slot_row = block_perm % frame_rows
    return (slot_frame, slot_row)


def rope_angles(frame_of_block, row_of_block, block_width, head_size):
    grid_shape = (frame_of_block.shape[0], block_width)
    pos_frame = (
        jnp.broadcast_to(frame_of_block[:, None], grid_shape).reshape(-1).astype(jnp.float32)
    )
    pos_row = jnp.broadcast_to(row_of_block[:, None], grid_shape).reshape(-1).astype(jnp.float32)
    pos_column = (
        jnp.broadcast_to(jnp.arange(block_width, dtype=jnp.int32)[None, :], grid_shape)
        .reshape(-1)
        .astype(jnp.float32)
    )
    pair_counts = (head_size // 16, 7 * head_size // 32, 7 * head_size // 32)
    angle_parts = []
    for position, pair_count in zip((pos_frame, pos_row, pos_column), pair_counts):
        frequency = ROPE_BASE ** (-jnp.arange(pair_count, dtype=jnp.float32) / pair_count)
        angle_parts.append(position[:, None] * frequency[None, :])
    return angle_parts


def normalize(vector):
    return vector * lax.rsqrt(jnp.mean(vector * vector, axis=-1, keepdims=True) + EPSILON)


def rotate(vector, angle_parts):
    pieces = []
    offset = 0
    for angle_part in angle_parts:
        pair_count = angle_part.shape[1]
        lower_half = vector[..., offset : offset + pair_count]
        upper_half = vector[..., offset + pair_count : offset + 2 * pair_count]
        cosine = jnp.cos(angle_part)[:, None, :]
        sine_part = jnp.sin(angle_part)[:, None, :]
        pieces.append(lower_half * cosine - upper_half * sine_part)
        pieces.append(lower_half * sine_part + upper_half * cosine)
        offset = offset + 2 * pair_count
    return jnp.concatenate(pieces, axis=-1)


def block_allowed(query_frame, key_frame):
    return (key_frame[None, :] <= query_frame[:, None]).astype(jnp.float32)


def attend(queries, key_data, value_data, allowed):
    query_len, head_count, head_size = queries.shape
    key_len = key_data.shape[0]
    key_heads = key_data.reshape(key_len, head_count, head_size)
    value_heads = value_data.reshape(key_len, head_count, head_size)
    scores = jnp.einsum(
        "qhd,khd->hqk", queries, key_heads, preferred_element_type=jnp.float32
    ) * head_size ** (-0.5)
    query_blocks, key_blocks = allowed.shape
    block_width = query_len // query_blocks
    token_ok = jnp.broadcast_to(
        allowed[:, None, :, None], (query_blocks, block_width, key_blocks, block_width)
    ).reshape(query_len, key_len)
    weights = jnp.exp(scores) * token_ok[None]
    denominator = jnp.sum(weights, axis=2).T
    numerator = jnp.einsum(
        "hqk,khd->qhd",
        weights.astype(jnp.bfloat16),
        value_heads,
        preferred_element_type=jnp.float32,
    )
    return (numerator, denominator)


def group_size(shards, tok_rows):
    fitting = [
        factor
        for factor in range(1, shards + 1)
        if shards % factor == 0 and factor * tok_rows >= 512
    ]
    return fitting[0]


def accumulate(totals, query_block, query_frame, key_block, value_block, key_frame):
    allowed = block_allowed(query_frame, key_frame)
    numerator, denominator = attend(query_block, key_block, value_block, allowed)
    return (totals[0] + numerator, totals[1] + denominator)


def per_device(tokens, w_qkv, w_out, block_perm):
    whole = gather_directly(tokens, "head", 1)
    tok_rows = whole.shape[0]
    local_blocks = tok_rows // WW
    head_count = w_qkv.shape[2] // HD
    slot_frame, slot_row = frames_and_rows(block_perm, F)
    first_slot = lax.axis_index("ctx") * local_blocks
    own_frame = lax.dynamic_slice_in_dim(slot_frame, first_slot, local_blocks)
    own_row = lax.dynamic_slice_in_dim(slot_row, first_slot, local_blocks)
    angle_parts = rope_angles(own_frame, own_row, WW, HD)
    query_raw = jnp.dot(whole, w_qkv[0], preferred_element_type=jnp.float32).reshape(
        tok_rows, head_count, HD
    )
    key_raw = jnp.dot(whole, w_qkv[1], preferred_element_type=jnp.float32).reshape(
        tok_rows, head_count, HD
    )
    value_data = jnp.dot(whole, w_qkv[2], preferred_element_type=jnp.float32).astype(jnp.bfloat16)
    queries = rotate(normalize(query_raw), angle_parts).astype(jnp.bfloat16)
    key_data = (
        rotate(normalize(key_raw), angle_parts)
        .astype(jnp.bfloat16)
        .reshape(tok_rows, head_count * HD)
    )
    start_totals = (
        jnp.zeros((tok_rows, head_count, HD), jnp.float32),
        jnp.zeros((tok_rows, head_count), jnp.float32),
    )
    totals = start_totals
    key_piece = lax.all_gather(key_data, "ctx", axis=0, tiled=True)
    value_piece = lax.all_gather(value_data, "ctx", axis=0, tiled=True)
    key_span = key_piece.shape[0]
    group = group_size(key_span // tok_rows, tok_rows)
    sub_span = group * tok_rows
    turns = key_span // sub_span

    def scan_step(running, packed):
        turn_id, key_block, value_block = packed
        key_frame = lax.dynamic_slice_in_dim(slot_frame, turn_id * sub_span // WW, sub_span // WW)
        return (accumulate(running, queries, own_frame, key_block, value_block, key_frame), None)

    totals, unused = lax.scan(
        scan_step,
        totals,
        (
            jnp.arange(turns, dtype=jnp.int32),
            key_piece.reshape(turns, sub_span, -1),
            value_piece.reshape(turns, sub_span, -1),
        ),
    )
    numerator, denominator = totals
    attention = (numerator / denominator[:, :, None]).astype(jnp.bfloat16)
    partial_out = jnp.dot(
        attention.reshape(tok_rows, head_count * HD), w_out, preferred_element_type=jnp.float32
    )
    mixed = sum_at_owner(partial_out.astype(jnp.bfloat16), "head", 1)
    return mixed.astype(jnp.bfloat16)


def solution(mesh):
    in_specs = (P("ctx", "head"), P(None, None, "head"), P("head", None), P())
    out_specs = P("ctx", "head")
    return jax.shard_map(
        per_device, mesh=mesh, in_specs=in_specs, out_specs=out_specs, check_vma=False
    )
```

profile of v0, /device:TPU:0, one launch (start us, length us, event | category | flops | bytes accessed | tf_op | source)
XLA Modules:
  0.0 320.8 jit_solution(5554707800320893478)
XLA Ops:
  6.5 1.1 broadcast_in_dim.34
  7.6 25.9 %all_to_all.10 = bf16[4,256,768]{2,1,0:T(8,128)(2,1)S(1)} all-to-all(bf16[4,256,768]{2,1,0:T(8,128)(2,1)S(1)} %broadcast_in_dim.34), channel_id=1, replica_groups=mesh['ctx'=32,'head'=4] {'head'}, dimensions={0} | all-to-all | bytes 3145728 | tf_op jit(solution)/shard_map/all_to_all | solution.py:17
  33.8 4.5 %fusion.16 = bf16[256,768]{1,0:T(8,128)(2,1)} fusion(bf16[256,3072]{1,0:T(8,128)(2,1)S(1)} %bitcast.92, bf16[3,3072,768]{2,1,0:T(8,128)(2,1)} %param.7), kind=kOutput, calls=%fused_computation.20 | convolution fusion | flops 1208156160 | bytes 6684672 | tf_op jit(solution)/shard_map/dot_general | solution.py:149
  39.0 8.0 %slice_bitcast_fusion = (bf16[768,3072]{0,1:T(8,128)(2,1)}, bf16[768,3072]{0,1:T(8,128)(2,1)}) fusion(bf16[3,3072,768]{2,1,0:T(8,128)(2,1)} %param.7), kind=kLoop, calls=%fused_computation.15 | loop fusion | bytes 18874368 | tf_op jit(solution)/shard_map/dot_general | solution.py:143
  47.0 6.7 %copy.30 = bf16[768,3072]{1,0:T(8,128)(2,1)} copy(bf16[768,3072]{0,1:T(8,128)(2,1)} %get-tuple-element.212) | data formatting | bytes 9437184 | tf_op jit(solution)/shard_map/dot_general | solution.py:143
  53.7 6.7 %copy.28 = bf16[768,3072]{1,0:T(8,128)(2,1)} copy(bf16[768,3072]{0,1:T(8,128)(2,1)} %get-tuple-element.213) | data formatting | bytes 9437184 | tf_op jit(solution)/shard_map/dot_general | solution.py:146
  60.8 1.2 copy.27
  62.1 2.1 reshape.268
  64.2 4.4 %multiply_reduce_fusion = (f32[256,6]{0,1:T(8,128)S(1)}, f32[256,6,128]{0,2,1:T(8,128)S(1)}) fusion(bf16[256,3072,1]{1,0,2:T(8,128)(2,1)} %reshape.268, bf16[6,128,3072]{2,1,0:T(8,128)(2,1)} %bitcast.90), kind=kOutput, calls=%fused_computation.22 | convolution fusion | flops 1208351232 | bytes 7084032 | tf_op jit(solution)/shard_map/dot_general | solution.py:143
  68.7 1.4 multiply_reduce_fusion.1
  72.6 28.0 %all-gather.3.cloned.1.call-done = bf16[8192,768]{1,0:T(8,128)(2,1)} async-done(((bf16[256,768]{1,0:T(8,128)(2,1)}), bf16[8192,768]{1,0:T(8,128)(2,1)}) %all-gather.3.cloned.1.call-update) | async-done | bytes 12582928 | tf_op jit(solution)/shard_map/all_gather | solution.py:162
  100.7 64.6 %all-gather.5.cloned.1.call-done = bf16[8192,768]{1,0:T(8,128)(2,1)} async-done(((bf16[256,768]{1,0:T(8,128)(2,1)}), bf16[8192,768]{1,0:T(8,128)(2,1)}) %all-gather.5.cloned.1.call-update) | async-done | bytes 12582928 | tf_op jit(solution)/shard_map/all_gather | solution.py:161
  165.2 117.2 %while.15 = (s32[]{:T(128)}, f32[256,6,128]{0,2,1:T(8,128)}, f32[256,6]{0,1:T(8,128)S(1)}, bf16[16,512,768]{2,1,0:T(8,128)(2,1)}, bf16[16,512,768]{2,1,0:T(8,128...) while((s32[]{:T(128)}, f32[256,6,128]{0,2,1:T(8,128)}, ...), condition=%wide.region_4.5_spmd.clone, body=%wide.region_2.4_spmd.clone.sunk | while | flops 407766592 | bytes 25060136 | solution.py:173
  167.5 1.5 constant_dynamic-slice_fusion.3
  171.6 0.9 copy-done.1
  174.8 1.5 constant_dynamic-slice_fusion.3
  179.0 0.9 copy-done.1
  182.1 1.5 constant_dynamic-slice_fusion.3
  186.3 0.9 copy-done.1
  189.5 1.5 constant_dynamic-slice_fusion.3
  193.6 0.9 copy-done.1
  196.8 1.5 constant_dynamic-slice_fusion.3
  200.9 0.9 copy-done.1
  204.1 1.5 constant_dynamic-slice_fusion.3
  208.3 0.9 copy-done.1
  211.4 1.5 constant_dynamic-slice_fusion.3
  215.6 0.9 copy-done.1
  218.8 1.5 constant_dynamic-slice_fusion.3
  222.9 0.9 copy-done.1
  226.1 1.5 constant_dynamic-slice_fusion.3
  230.2 0.9 copy-done.1
  233.4 1.5 constant_dynamic-slice_fusion.3
  237.6 0.9 copy-done.1
  240.7 1.5 constant_dynamic-slice_fusion.3
  244.9 0.9 copy-done.1
  248.1 1.5 constant_dynamic-slice_fusion.3
  252.2 0.9 copy-done.1
  255.4 1.5 constant_dynamic-slice_fusion.3
  259.5 0.9 copy-done.1
  262.7 1.5 constant_dynamic-slice_fusion.3
  266.9 0.9 copy-done.1
  270.1 1.5 constant_dynamic-slice_fusion.3
  274.2 0.9 copy-done.1
  277.4 1.5 constant_dynamic-slice_fusion.3
  282.5 1.2 divide_convert_fusion
  283.7 3.8 %convolution_convert_fusion = bf16[256,3072]{1,0:T(8,128)(2,1)S(1)} fusion(bf16[256,768]{0,1:T(8,128)(2,1)S(1)} %bitcast.91, bf16[768,3072]{1,0:T(8,128)(2,1)} %param.8), kind=kOutput, calls=%fused_computation.18 | convolution fusion | flops 1208745984 | bytes 6684672 | tf_op jit(solution)/shard_map/dot_general | solution.py:184
  287.5 25.3 %all_to_all.11 = bf16[4,256,768]{2,1,0:T(8,128)(2,1)S(1)} all-to-all(bf16[4,256,768]{2,1,0:T(8,128)(2,1)S(1)} %bitcast.86), channel_id=1, replica_groups=mesh['ctx'=32,'head'=4] {'head'}, dimensions={0} | all-to-all | bytes 3145728 | tf_op jit(solution)/shard_map/all_to_all | solution.py:41
  312.9 1.1 reduce_sum.44
  (250 shorter events, 71.4 us)
Async XLA Ops:
  6.5 94.1 %all-gather.3.cloned.1.call-start = ((), (), s32[]{:S(2)}) async-start(), calls=%async_computation.2 | async-start | bytes 12976128 | tf_op jit(solution)/shard_map/all_gather | solution.py:162
  33.8 4.6 %copy-start.3 = (s32[128]{0:T(128)S(1)}, s32[128]{0:T(128)}, u32[]{:S(2)}) copy-start(s32[128]{0:T(128)} %param.9) | copy-start | bytes 1540
  38.3 126.9 %all-gather.5.cloned.1.call-start = ((), (), s32[]{:S(2)}) async-start(), calls=%async_computation.3 | async-start | bytes 12976128 | tf_op jit(solution)/shard_map/all_gather | solution.py:161
  62.1 6.5 %slice-start = ((s8[4718592]{0:T(1024)(128)(4,1)}), s8[524288]{0:T(1024)(128)(4,1)S(1)}, s32[]{:S(2)}) async-start(s8[4718592]{0:T(1024)(128)(4,1)} %bitcast.87), calls=%async_computation.4 | async-start | bytes 1048576
  64.2 4.4 %slice-start.1 = ((s8[4718592]{0:T(1024)(128)(4,1)}), s8[4194304]{0:T(1024)(128)(4,1)S(1)}, s32[]{:S(2)}) async-start(s8[4718592]{0:T(1024)(128)(4,1)} %bitcast.87), calls=%async_computation.5 | async-start | bytes 8388608
  64.2 4.5 %copy-start.2 = (bf16[256,3072,1]{1,0,2:T(8,128)(2,1)S(1)}, bf16[256,3072,1]{1,0,2:T(8,128)(2,1)}, u32[]{:S(2)}) copy-start(bf16[256,3072,1]{1,0,2:T(8,128)(2,1)} %reshape.268) | copy-start | bytes 4718596
  169.5 1.1 copy-start
  171.6 1.0 copy-start.1
  176.9 1.1 copy-start
  178.9 1.0 copy-start.1
  184.2 1.1 copy-start
  186.3 1.0 copy-start.1
  191.5 1.1 copy-start
  193.6 1.0 copy-start.1
  198.8 1.1 copy-start
  200.9 1.0 copy-start.1
  206.2 1.1 copy-start
  208.2 1.0 copy-start.1
  213.5 1.1 copy-start
  215.6 1.0 copy-start.1
  220.8 1.1 copy-start
  222.9 1.0 copy-start.1
  228.1 1.1 copy-start
  230.2 1.0 copy-start.1
  235.5 1.1 copy-start
  237.5 1.0 copy-start.1
  242.8 1.1 copy-start
  244.9 1.0 copy-start.1
  250.1 1.1 copy-start
  252.2 1.0 copy-start.1
  257.5 1.1 copy-start
  259.5 1.0 copy-start.1
  264.8 1.1 copy-start
  266.8 1.0 copy-start.1
  272.1 1.1 copy-start
  274.2 1.0 copy-start.1
  279.4 1.1 copy-start
  281.5 1.0 copy-start.1
Sparse Core Ops, SparseCore 0:
  38.4 62.1 all-gather.2
  102.9 62.2 all-gather.4
where the time goes:
time: 323 us; the launch traced here: 321 us
  local copies, waits for them, and re-layouts  104 us (32%)
  waiting for transfers between devices  92.6 us (29%)
  blocking collectives  51.3 us (16%)
  matrix products  42.7 us (13%)
  between operations  13.6 us (4%)
  loops' own time  11.9 us (4%)
  other arithmetic  4.6 us (1%)
    all_gather x1, waiting for transfers between devices, per_device(): key_piece = lax.all_gather(key_data, 'ctx', axis=0, tiled=True)  64.6 us
    dynamic_slice x64, local copies, waits for them, and re-layouts, per_device(): lax.scan(scan_step, totals, (jnp.arange(turns, dtype=jnp.int32), key_piec...  41.9 us
    all_gather x1, waiting for transfers between devices, per_device(): value_piece = lax.all_gather(value_data, 'ctx', axis=0, tiled=True)  28 us
    all_to_all x1, blocking collectives, from_everyone(): lax.all_to_all(jnp.broadcast_to(shard[None], (count, *shard.shape)), axis...  25.9 us
    all_to_all x1, blocking collectives, sum_at_owner(): lax.all_to_all(parts, axis, split_axis=0, concat_axis=0, tiled=True)  25.3 us
    while x64, local copies, waits for them, and re-layouts  19.2 us
    dot_general x16, matrix products, attend(): jnp.einsum('hqk,khd->qhd', weights.astype(jnp.bfloat16), value_heads, pre...  14.8 us
    dot_general x2, local copies, waits for them, and re-layouts, per_device(): jnp.dot(whole, w_qkv[0], preferred_element_type=jnp.float32)  14.8 us
  transfers between devices with their start and end apart: 2, of which 2 were waited for; matrix products, arithmetic and copies ran while one was open for 11% of the time, Pallas kernels for 0%

commit v1 on v0

v1 whole, which is shorter than its diff:
```python
import functools
import math

import jax
import jax.numpy as jnp
import numpy as np
from jax import lax
from jax.experimental import pallas as pl
from jax.experimental.pallas import tpu as pltpu
from jax.sharding import PartitionSpec as P

HD = 128
WW = 64
ROPE_BASE = 10000.0
EPSILON = 1e-06
N = 4
R = 128
HH = 3
HW = HH * HD
DW = 2 * HW
OB = R + 8
BF = jnp.bfloat16
F32 = jnp.float32
RIGHT, LEFT = 0, 1
STEP = (1, N - 1)


def rope_tables(frame_rows):
    parts = ((0, HD // 16), (HD // 8, 7 * HD // 32), (HD // 8 + 7 * HD // 16, 7 * HD // 32))
    frames = np.arange(128) // frame_rows
    rows = np.arange(128) % frame_rows
    tables = []
    for position, kinds in ((np.stack([frames, rows]), (0, 1)), (np.arange(WW)[None], (2,))):
        cosine = np.zeros((position.shape[1], HD), np.float32)
        sine = np.zeros((position.shape[1], HD), np.float32)
        for at, kind in enumerate(kinds):
            first, pairs = parts[kind]
            freq = np.float32(ROPE_BASE) ** (-np.arange(pairs, dtype=np.float32) / pairs)
            angle = position[at].astype(np.float32)[:, None] * freq[None, :].astype(np.float32)
            cosine[:, first : first + pairs] = np.cos(angle)
            cosine[:, first + pairs : first + 2 * pairs] = np.cos(angle)
            sine[:, first : first + pairs] = -np.sin(angle)
            sine[:, first + pairs : first + 2 * pairs] = np.sin(angle)
        tables += [cosine, sine]
    return tables


def kernel(
    perm, frc, frs, coc, cos_, tok, wqkv, wout, out,
    xg, wq, wo, acc, cost, sint, okv, oq, kv, qb, num, den,
    os1, or1, os2, or2, oss, ors, attn, zs1, zr1, zp, zs2, zr2,
    lsem, gs, gr, xs, xr, o1s, o1r, o2s, o2r, oqs, oqr, zss, zsr,
):
    ctx = lax.axis_index("ctx")
    z = lax.axis_index("head")
    c = ctx % 2
    x = (ctx // 2) % N
    y = ctx // (2 * N)

    def cid(yy, xx, cc):
        return (yy * N + xx) * 2 + cc

    def kv_to(half, d):
        if half == 0:
            return cid(y, (x + d) % N, 0)
        return cid((y + d) % N, x, 1)

    def q_to(half, d):
        if half == 0:
            return cid((y + d) % N, x, 0)
        return cid(y, (x + d) % N, 1)

    def my_kv(d):
        return cid((y + c * d) % N, (x + (1 - c) * d) % N, c)

    def my_q(d, core):
        return cid((y + (1 - c) * d) % N, (x + c * d) % N, core)

    sibling = cid(y, x, 1 - c)
    kc = x * (1 - c) + y * c
    qc = y * (1 - c) + x * c
    pending = []

    def send(src, dst, ss, rs, to_ctx, to_z):
        copy = pltpu.make_async_remote_copy(
            src_ref=src, dst_ref=dst, send_sem=ss, recv_sem=rs,
            device_id=(to_ctx, to_z), device_id_type=pl.DeviceIdType.MESH,
        )
        copy.start()
        pending.append(copy)

    def arrive(dst, rs):
        pltpu.make_async_remote_copy(
            src_ref=dst, dst_ref=dst, send_sem=rs, recv_sem=rs,
            device_id=(sibling, z), device_id_type=pl.DeviceIdType.MESH,
        ).wait_recv()

    tok_in = [
        pltpu.make_async_copy(tok.at[pl.ds(h * R, R)], xg.at[h, z], lsem.at[h]) for h in range(2)
    ]
    for copy in tok_in:
        copy.start()
    rel_order = (0, 3, 1, 2)
    w_in = []
    for at, rel in enumerate(rel_order):
        rows = pl.ds(pl.multiple_of((z + rel) % N * DW, DW), DW)
        for j in range(3):
            w_in.append(
                pltpu.make_async_copy(wqkv.at[j, rows], wq.at[j, rows], lsem.at[2 + at * 3 + j])
            )
    for copy in w_in:
        copy.start()
    wo_in = pltpu.make_async_copy(wout, wo, lsem.at[14])
    wo_in.start()

    barrier = pltpu.get_barrier_semaphore()
    peers = [(sibling, z)]
    for d in STEP:
        peers.append((ctx, (z + d) % N))
        for core in range(2):
            peers.append((cid(y, (x + d) % N, core), z))
            peers.append((cid((y + d) % N, x, core), z))
    for peer in peers:
        pl.semaphore_signal(barrier, inc=1, device_id=peer, device_id_type=pl.DeviceIdType.MESH)
    pl.semaphore_wait(barrier, len(peers))

    def gather_own(h):
        for way in (RIGHT, LEFT):
            send(xg.at[h, z], xg.at[h, z], gs.at[h, way], gr.at[h, way], ctx, (z + STEP[way]) % N)

    def gather_relay(h):
        left, right = (z + 3) % N, (z + 1) % N
        arrive(xg.at[h, left], gr.at[h, RIGHT])
        lo, hi = pl.ds(0, R // 2), pl.ds(R // 2, R // 2)
        send(xg.at[h, left, lo], xg.at[h, left, lo], gs.at[h, 2], gr.at[h, 2], ctx, right)
        arrive(xg.at[h, right], gr.at[h, LEFT])
        send(xg.at[h, right, hi], xg.at[h, right, hi], gs.at[h, 3], gr.at[h, 3], ctx, left)

    def gather_last(h):
        far = (z + 2) % N
        arrive(xg.at[h, far, pl.ds(0, R // 2)], gr.at[h, 2])
        arrive(xg.at[h, far, pl.ds(R // 2, R // 2)], gr.at[h, 3])

    def weights(at):
        for j in range(3):
            w_in[at * 3 + j].wait()

    def project(hs, rel, first):
        src = (z + rel) % N
        rows = pl.ds(pl.multiple_of(src * DW, DW), DW)

        def tile(t, carry):
            cols = pl.ds(pl.multiple_of(t % 3 * 256, 256), 256)
            at = pl.ds(pl.multiple_of(t * 256, 256), 256)
            w = wq[t // 3, rows, cols]
            if len(hs) == 2:
                a = jnp.concatenate([xg[h, src] for h in hs], axis=0)
            else:
                a = xg[hs[0], src]
            part = jnp.dot(a, w, preferred_element_type=F32)
            for n, h in enumerate(hs):
                piece = part[n * R : (n + 1) * R]
                if first:
                    acc[h, :, at] = piece
                else:
                    acc[h, :, at] += piece
            return carry

        lax.fori_loop(0, 9, tile, 0)

    def tables():
        for s in range(4):
            at = perm[4 * ctx + s]
            rows = pl.ds(s * WW, WW)
            cost[rows, :] = frc[pl.ds(at, 1), :] + coc[...]
            sint[rows, :] = frs[pl.ds(at, 1), :] + cos_[...]

    def finish(h):
        rows = pl.ds(h * R, R)
        lane = lax.broadcasted_iota(jnp.int32, (R, HD), 1)
        wide = lane >= 16
        low = (lane < 8) | ((lane >= 16) & (lane < 44)) | ((lane >= 72) & (lane < 100))

        def turned(v, scale):
            square = jnp.mean(v * v, axis=-1, keepdims=True)
            v = v * (lax.rsqrt(square + EPSILON) * scale)
            up = jnp.where(wide, pltpu.roll(v, HD - 28, 1), pltpu.roll(v, HD - 8, 1))
            down = jnp.where(wide, pltpu.roll(v, 28, 1), pltpu.roll(v, 8, 1))
            return (v * cost[rows, :] + jnp.where(low, up, down) * sint[rows, :]).astype(BF)

        for half in range(2):
            for i in range(HH):
                to = pl.ds(i * HD, HD)
                col = (half * HH + i) * HD
                oq[half, h, :, to] = turned(acc[h, :, pl.ds(col, HD)], HD**-0.5 / math.log(2.0))
                okv[half, h, :, to] = turned(acc[h, :, pl.ds(DW + col, HD)], 1.0)
                okv[half, h, :, pl.ds(HW + i * HD, HD)] = acc[h, :, pl.ds(2 * DW + col, HD)].astype(
                    BF
                )

    def spread(h):
        for half in range(2):
            kslot, qslot = ((x, y), (y, x))[half]
            for way in (RIGHT, LEFT):
                send(
                    oq.at[half, h], qb.at[h, qslot, c], xs.at[1, h, half * 2 + way],
                    xr.at[1, h, 1 + 2 * way + c], q_to(half, STEP[way]), z,
                )
                send(
                    okv.at[half, h], kv.at[h, kslot, c], xs.at[0, h, half * 2 + way],
                    xr.at[0, h, 1 + 2 * way + c], kv_to(half, STEP[way]), z,
                )
        send(okv.at[1 - c, h], kv.at[h, qc, c], xs.at[0, h, 4], xr.at[0, h, 0], sibling, z)
        send(oq.at[1 - c, h], qb.at[h, kc, c], xs.at[1, h, 4], xr.at[1, h, 0], sibling, z)
        kv[h, kc, c] = okv[c, h]
        qb[h, qc, c] = oq[c, h]

    def spread_relay(h):
        for way in (RIGHT, LEFT):
            kslot = (kc + N - STEP[way]) % N
            qslot = (qc + N - STEP[way]) % N
            for core in range(2):
                arrive(qb.at[h, qslot, core], xr.at[1, h, 1 + 2 * way + core])
            send(
                qb.at[h, qslot, way], qb.at[h, qslot, way], xs.at[1, h, 5 + way],
                xr.at[1, h, 5 + way], my_q(STEP[way], c), z,
            )
            for core in range(2):
                arrive(kv.at[h, kslot, core], xr.at[0, h, 1 + 2 * way + core])
            send(
                kv.at[h, kslot, way], kv.at[h, kslot, way], xs.at[0, h, 5 + way],
                xr.at[0, h, 5 + way], my_kv(STEP[way]), z,
            )
        arrive(kv.at[h, kc, 1 - c], xr.at[0, h, 0])
        arrive(qb.at[h, qc, 1 - c], xr.at[1, h, 0])

    def spread_last(h):
        for way in (RIGHT, LEFT):
            arrive(qb.at[h, (qc + 2) % N, way], xr.at[1, h, 5 + way])
            arrive(kv.at[h, (kc + 2) % N, way], xr.at[0, h, 5 + way])

    frame_rows = perm.shape[0] // 8

    def attend(hq, hk, rel, masked, first):
        slot = (qc + rel) % N
        if masked:
            fq = [
                perm[4 * cid((1 - c) * slot + c * y, (1 - c) * x + c * slot, a) + 2 * hq] // frame_rows
                for a in range(2)
            ]
            fk = [
                perm[4 * cid((1 - c) * y + c * t, (1 - c) * t + c * x, b) + 2 * hk] // frame_rows
                for t in range(N)
                for b in range(2)
            ]
            ok = [[(k <= q).astype(F32) for k in fk] for q in fq]

        for i in range(HH):
            cols = pl.ds(i * HD, HD)
            vcols = pl.ds(HW + i * HD, HD)
            q = qb[hq, slot, :, :, cols].reshape(2 * R, HD)
            k = kv[hk, :, :, :, cols].reshape(2 * N * R, HD)
            v = kv[hk, :, :, :, vcols].reshape(2 * N * R, HD)
            s = lax.dot_general(q, k, (((1,), (1,)), ((), ())), preferred_element_type=F32)
            w = jnp.exp2(s)
            if masked:
                w = jnp.concatenate(
                    [
                        jnp.concatenate(
                            [
                                w[a * R : (a + 1) * R, b * R : (b + 1) * R] * ok[a][b]
                                for b in range(2 * N)
                            ],
                            axis=1,
                        )
                        for a in range(2)
                    ],
                    axis=0,
                )
            total = w[:, :HD]
            for b in range(1, 2 * N):
                total = total + w[:, b * HD : (b + 1) * HD]
            o = jnp.dot(w.astype(BF), v, preferred_element_type=F32)
            for a in range(2):
                rows = slice(a * R, (a + 1) * R)
                if first:
                    num[hq, slot, a, :, cols] = o[rows]
                    den[hq, slot, a, :, cols] = total[rows]
                else:
                    num[hq, slot, a, :, cols] += o[rows]
                    den[hq, slot, a, :, cols] += total[rows]

    def row_sum(h, slot, core, i):
        return jnp.sum(den[h, slot, core, :, pl.ds(i * HD, HD)].T, axis=0, keepdims=True)

    def pack(dst, h, slot, core, plus=None):
        for i in range(HH):
            cols = pl.ds(i * HD, HD)
            n = num[h, slot, core, :, cols]
            d = row_sum(h, slot, core, i)
            if plus is not None:
                n = n + plus[pl.ds(0, R), cols].astype(F32)
                d = d + plus[pl.ds(R, 8), cols].astype(F32)
            dst[pl.ds(0, R), cols] = n.astype(BF)
            dst[pl.ds(R, 8), cols] = jnp.broadcast_to(d, (8, HD)).astype(BF)

    def sum_far(h):
        far = (qc + 2) % N
        for way in (RIGHT, LEFT):
            pack(os1.at[h, way], h, far, way)
            send(
                os1.at[h, way], or1.at[h, way], o1s.at[h, way], o1r.at[h, way],
                my_q(STEP[way], c), z,
            )

    def sum_near(h):
        for way in (RIGHT, LEFT):
            slot = (qc + STEP[way]) % N
            arrive(or1.at[h, way], o1r.at[h, way])
            for core in range(2):
                pack(os2.at[h, way, core], h, slot, core, or1.at[h, way] if core == way else None)
                send(
                    os2.at[h, way, core], or2.at[h, c, way], o2s.at[h, way, core],
                    o2r.at[h, c, way], my_q(STEP[way], core), z,
                )

    def sum_sibling(h):
        pack(oss.at[h], h, qc, 1 - c)
        send(oss.at[h], ors.at[h], oqs.at[h], oqr.at[h], sibling, z)

    def normalize(h):
        for half in range(2):
            for way in (RIGHT, LEFT):
                arrive(or2.at[h, half, way], o2r.at[h, half, way])
        arrive(ors.at[h], oqr.at[h])
        for mine in range(2):
            half = c if mine else 1 - c
            for i in range(HH):
                cols = pl.ds(i * HD, HD)
                if mine:
                    n = num[h, qc, c, :, cols]
                    d = row_sum(h, qc, c, i)
                else:
                    n = ors[h, pl.ds(0, R), cols].astype(F32)
                    d = ors[h, pl.ds(R, 8), cols].astype(F32)[:1]
                for way in (RIGHT, LEFT):
                    n = n + or2[h, half, way, pl.ds(0, R), cols].astype(F32)
                    d = d + or2[h, half, way, pl.ds(R, 8), cols].astype(F32)[:1]
                attn[h, half, :, cols] = (n / jnp.broadcast_to(d, (HD, R)).T).astype(BF)

    def mixed_for(h, rel, store):
        base = (z + rel) % N * DW

        for t in range(3):
            cols = pl.ds(pl.multiple_of(base + t * 256, 256), 256)
            part = jnp.dot(attn[h, 0], wo[pl.ds(0, HW), cols], preferred_element_type=F32)
            part += jnp.dot(attn[h, 1], wo[pl.ds(HW, HW), cols], preferred_element_type=F32)
            store(pl.ds(t * 256, 256), part)

    def mix_far(h):
        def store(cols, part):
            zs1[h, RIGHT, :, cols] = part[: R // 2].astype(BF)
            zs1[h, LEFT, :, cols] = part[R // 2 :].astype(BF)

        mixed_for(h, 2, store)
        for way in (RIGHT, LEFT):
            send(
                zs1.at[h, way], zr1.at[h, way], zss.at[h, 0, way], zsr.at[h, 0, way],
                ctx, (z + STEP[way]) % N,
            )

    def mix_rest(h):
        for at, rel in enumerate((1, 3, 0)):

            def store(cols, part, at=at):
                zp[h, at, :, cols] = part

            mixed_for(h, rel, store)

    def mix_near(h):
        lo, hi = pl.ds(0, R // 2), pl.ds(R // 2, R // 2)
        for way in (RIGHT, LEFT):
            summed, plain = ((lo, hi), (hi, lo))[way]
            zs2[h, way, plain] = zp[h, way, plain].astype(BF)
            arrive(zr1.at[h, way], zsr.at[h, 0, way])
            zs2[h, way, summed] = (zp[h, way, summed] + zr1[h, way].astype(F32)).astype(BF)
            send(
                zs2.at[h, way], zr2.at[h, way], zss.at[h, 1, way], zsr.at[h, 1, way],
                ctx, (z + STEP[way]) % N,
            )

    def mix_last(h):
        total = zp[h, 2]
        for way in (RIGHT, LEFT):
            arrive(zr2.at[h, way], zsr.at[h, 1, way])
            total = total + zr2[h, way].astype(F32)
        out[pl.ds(h * R, R), :] = total.astype(BF)

    tok_in[0].wait()
    gather_own(0)
    tok_in[1].wait()
    tables()
    weights(0)
    project((0, 1), 0, True)
    gather_relay(0)
    gather_own(1)
    weights(1)
    project((0,), 3, False)
    weights(2)
    project((0,), 1, False)
    weights(3)
    gather_last(0)
    project((0,), 2, False)
    finish(0)
    spread(0)
    gather_relay(1)
    project((1,), 3, False)
    project((1,), 1, False)
    gather_last(1)
    project((1,), 2, False)
    finish(1)
    spread_relay(0)
    spread(1)
    spread_last(0)
    attend(0, 0, 2, True, True)
    sum_far(0)
    for rel in (1, 3, 0):
        attend(0, 0, rel, True, True)
    spread_relay(1)
    sum_near(0)
    sum_sibling(0)
    for rel in (1, 3, 0):
        attend(1, 0, rel, False, True)
    wo_in.wait()
    normalize(0)
    mix_far(0)
    mix_rest(0)
    spread_last(1)
    attend(1, 0, 2, False, True)
    attend(1, 1, 2, True, False)
    sum_far(1)
    mix_near(0)
    for rel in (1, 3):
        attend(1, 1, rel, True, False)
    sum_near(1)
    attend(1, 1, 0, True, False)
    sum_sibling(1)
    mix_last(0)
    normalize(1)
    mix_far(1)
    mix_rest(1)
    mix_near(1)
    mix_last(1)
    for copy in pending:
        copy.wait_send()


def per_device(tokens, w_qkv, w_out, block_perm):
    frc, frs, coc, cos_ = [jnp.asarray(t) for t in rope_tables(block_perm.shape[0] // 8)]
    vmem = pl.BlockSpec(memory_space=pltpu.VMEM)
    hbm = pl.BlockSpec(memory_space=pl.ANY)
    dma = pltpu.SemaphoreType.DMA
    return pl.pallas_call(
        kernel,
        name="attention_layer",
        out_shape=jax.ShapeDtypeStruct((2 * R, DW), BF),
        in_specs=[pl.BlockSpec(memory_space=pltpu.SMEM)] + [vmem] * 4 + [hbm] * 3,
        out_specs=vmem,
        scratch_shapes=[
            pltpu.VMEM((2, N, R, DW), BF),
            pltpu.VMEM((3, N * DW, DW), BF),
            pltpu.VMEM((DW, N * DW), BF),
            pltpu.VMEM((2, R, 3 * DW), F32),
            pltpu.VMEM((2 * R, HD), F32),
            pltpu.VMEM((2 * R, HD), F32),
            pltpu.VMEM((2, 2, R, DW), BF),
            pltpu.VMEM((2, 2, R, HW), BF),
            pltpu.VMEM((2, N, 2, R, DW), BF),
            pltpu.VMEM((2, N, 2, R, HW), BF),
            pltpu.VMEM((2, N, 2, R, HW), F32),
            pltpu.VMEM((2, N, 2, R, HW), F32),
            pltpu.VMEM((2, 2, OB, HW), BF),
            pltpu.VMEM((2, 2, OB, HW), BF),
            pltpu.VMEM((2, 2, 2, OB, HW), BF),
            pltpu.VMEM((2, 2, 2, OB, HW), BF),
            pltpu.VMEM((2, OB, HW), BF),
            pltpu.VMEM((2, OB, HW), BF),
            pltpu.VMEM((2, 2, R, HW), BF),
            pltpu.VMEM((2, 2, R // 2, DW), BF),
            pltpu.VMEM((2, 2, R // 2, DW), BF),
            pltpu.VMEM((2, 3, R, DW), F32),
            pltpu.VMEM((2, 2, R, DW), BF),
            pltpu.VMEM((2, 2, R, DW), BF),
            dma((15,)),
            dma((2, 4)),
            dma((2, 4)),
            dma((2, 2, 7)),
            dma((2, 2, 7)),
            dma((2, 2)),
            dma((2, 2)),
            dma((2, 2, 2)),
            dma((2, 2, 2)),
            dma((2,)),
            dma((2,)),
            dma((2, 2, 2)),
            dma((2, 2, 2)),
        ],
        compiler_params=pltpu.CompilerParams(
            collective_id=0, has_side_effects=True, vmem_limit_bytes=64 * 1024 * 1024 - 65536
        ),
    )(block_perm, frc, frs, coc, cos_, tokens, w_qkv, w_out)


def solution(mesh):
    in_specs = (P("ctx", "head"), P(None, None, "head"), P("head", None), P())
    return jax.shard_map(
        per_device, mesh=mesh, in_specs=in_specs, out_specs=P("ctx", "head"), check_vma=False
    )
```

time: 323 us -> 78.5 us (0.24)
  local copies, waits for them, and re-layouts: 104 us -> 1.77 us
  waiting for transfers between devices: 92.6 us -> 0 us
  Pallas kernels: 0 us -> 75.9 us
  blocking collectives: 51.3 us -> 0 us
  matrix products: 42.7 us -> 0 us
  between operations: 13.6 us -> 0.01 us
  loops' own time: 11.9 us -> 0 us
  other arithmetic: 4.6 us -> 0 us
    all_gather x2 -> x0, waiting for transfers between devices: 92.6 us -> none  [the longest x1 64.6 us: per_device(): key_piece = lax.all_gather(key_data, 'ctx', axis=0, tiled=True)]
    pallas_call x0 -> x1, Pallas kernels: none -> 75.9 us  [per_device(): pl.pallas_call(kernel, name='attention_layer', out_shape=jax.ShapeDtypeSt...]
    all_to_all x2 -> x0, blocking collectives: 51.3 us -> none  [the longest x1 25.9 us: from_everyone(): lax.all_to_all(jnp.broadcast_to(shard[None], (count, *shard.shape)), axis...]
    dynamic_slice x80 -> x0, local copies, waits for them, and re-layouts: 43.1 us -> none  [the longest x64 41.9 us: per_device(): lax.scan(scan_step, totals, (jnp.arange(turns, dtype=jnp.int32), key_piec...]
    dot_general x36 -> x0, matrix products: 42.7 us -> none  [the longest x16 14.8 us: attend(): jnp.einsum('hqk,khd->qhd', weights.astype(jnp.bfloat16), value_heads, pre...]
    dot_general x3 -> x0, local copies, waits for them, and re-layouts: 21.4 us -> none  [the longest x2 14.8 us: per_device(): jnp.dot(whole, w_qkv[0], preferred_element_type=jnp.float32)]
    while x64 -> x0, local copies, waits for them, and re-layouts: 19.2 us -> none
    another operation x1 -> x0, loops' own time: 11.9 us -> none  [per_device(): lax.scan(scan_step, totals, (jnp.arange(turns, dtype=jnp.int32), key_piec...]
  transfers between devices with their start and end apart: 2 -> 0, of which waited for: 2 -> 0; matrix products, arithmetic and copies ran while one was open for 11% -> 0% of each run, Pallas kernels for 0% -> 0%
where the time goes in v1:
time: 78.5 us; the launch traced here: 77.7 us
  Pallas kernels  75.9 us (97%)
  local copies, waits for them, and re-layouts  1.77 us (2%)
    pallas_call x1, Pallas kernels, per_device(): pl.pallas_call(kernel, name='attention_layer', out_shape=jax.ShapeDtypeSt...  75.9 us
    unnamed x1, local copies, waits for them, and re-layouts  1.77 us

profile of v1, /device:TPU:0, one launch (start us, length us, event | category | flops | bytes accessed | tf_op | source)
XLA Modules:
  0.0 77.7 jit_solution(5891706197124913331)
XLA Ops:
  0.0 75.9 %attention_layer.1 = bf16[256,768]{1,0:T(8,128)(2,1)} custom-call(s32[128]{0:T(128)} %perm.1, f32[128,128]{1,0:T(8,128)} %constant.8.clone.frc, f32[128,128]{1,0:T(8,128)} %constant.9.clone.frs, f32[64,128]{1,0:T(8,128)} %constant.10.clone.coc, f32[64,128]{1,0:T(8,128)} %constant.11.clone.cos_, bf16[256,768]{1,0:T(8,128)(2,1)} %tok.1, ...), custom_call_target="tpu_custom_call" | custom-call | tf_op jit(solution)/shard_map/attention_layer/pallas_call | solution.py:463
  75.9 1.8 %copy.10 = bf16[256,768]{1,0:T(8,128)(2,1)} copy(bf16[256,768]{1,0:T(8,128)(2,1)} %attention_layer.1) | data formatting | bytes 786432

commit v2 on v1

v2 whole, which is shorter than its diff:
```python
import functools
import math

import jax
import jax.numpy as jnp
import numpy as np
from jax import lax
from jax.experimental import pallas as pl
from jax.experimental.pallas import tpu as pltpu
from jax.sharding import PartitionSpec as P

HD = 128
WW = 64
ROPE_BASE = 10000.0
EPSILON = 1e-06
N = 4
R = 128
HH = 3
HW = HH * HD
DW = 2 * HW
OB = R + 8
BF = jnp.bfloat16
F32 = jnp.float32
RIGHT, LEFT = 0, 1
STEP = (1, N - 1)


def rope_tables(frame_rows):
    parts = ((0, HD // 16), (HD // 8, 7 * HD // 32), (HD // 8 + 7 * HD // 16, 7 * HD // 32))
    frames = np.arange(128) // frame_rows
    rows = np.arange(128) % frame_rows
    tables = []
    for position, kinds in ((np.stack([frames, rows]), (0, 1)), (np.arange(WW)[None], (2,))):
        cosine = np.zeros((position.shape[1], HD), np.float32)
        sine = np.zeros((position.shape[1], HD), np.float32)
        for at, kind in enumerate(kinds):
            first, pairs = parts[kind]
            freq = np.float32(ROPE_BASE) ** (-np.arange(pairs, dtype=np.float32) / pairs)
            angle = position[at].astype(np.float32)[:, None] * freq[None, :].astype(np.float32)
            cosine[:, first : first + pairs] = np.cos(angle)
            cosine[:, first + pairs : first + 2 * pairs] = np.cos(angle)
            sine[:, first : first + pairs] = -np.sin(angle)
            sine[:, first + pairs : first + 2 * pairs] = np.sin(angle)
        tables += [cosine, sine]
    return tables


def kernel(
    perm_hbm, tab_hbm, tok, wqkv, wout, out,
    perm, tab, xg, wq, wo, acc, cost, sint, swap, okv, oq, kv, qb, num, den,
    os1, or1, os2, or2, oss, ors, attn, zs1, zr1, zp, own, zs2, zr2, mixed,
    lsem, gs, gr, ks, kr, krs, krr, qs, qr, qrs, qrr, sbs, sbr,
    o1s, o1r, o2s, o2r, oqs, oqr, z1s, z1r, z2s, z2r,
):
    ctx = lax.axis_index("ctx")
    z = lax.axis_index("head")
    c = ctx % 2
    x = (ctx // 2) % N
    y = ctx // (2 * N)

    def cid(yy, xx, cc):
        return (yy * N + xx) * 2 + cc

    def kv_to(half, d):
        if half == 0:
            return cid(y, (x + d) % N, 0)
        return cid((y + d) % N, x, 1)

    def q_to(half, d):
        if half == 0:
            return cid((y + d) % N, x, 0)
        return cid(y, (x + d) % N, 1)

    def my_kv(d):
        return cid((y + c * d) % N, (x + (1 - c) * d) % N, c)

    def my_q(d, core):
        return cid((y + (1 - c) * d) % N, (x + c * d) % N, core)

    sibling = cid(y, x, 1 - c)
    kc = x * (1 - c) + y * c
    qc = y * (1 - c) + x * c
    pending = []

    def send(src, dst, ss, rs, to_ctx, to_z):
        copy = pltpu.make_async_remote_copy(
            src_ref=src, dst_ref=dst, send_sem=ss, recv_sem=rs,
            device_id=(to_ctx, to_z), device_id_type=pl.DeviceIdType.MESH,
        )
        copy.start()
        pending.append(copy)

    def arrive(dst, rs):
        pltpu.make_async_remote_copy(
            src_ref=dst, dst_ref=dst, send_sem=rs, recv_sem=rs,
            device_id=(sibling, z), device_id_type=pl.DeviceIdType.MESH,
        ).wait_recv()

    perm_in = pltpu.make_async_copy(perm_hbm, perm, lsem.at[15])
    perm_in.start()
    tab_in = pltpu.make_async_copy(tab_hbm, tab, lsem.at[16])
    tab_in.start()
    tok_in = [
        pltpu.make_async_copy(tok.at[pl.ds(h * R, R)], xg.at[h, z], lsem.at[h]) for h in range(2)
    ]
    for copy in tok_in:
        copy.start()
    rel_order = (0, 3, 1, 2)
    w_in = []
    for at, rel in enumerate(rel_order):
        rows = pl.ds(pl.multiple_of((z + rel) % N * DW, DW), DW)
        for j in range(3):
            w_in.append(
                pltpu.make_async_copy(wqkv.at[j, rows], wq.at[j, rows], lsem.at[2 + at * 3 + j])
            )
    for copy in w_in:
        copy.start()
    wo_in = pltpu.make_async_copy(wout, wo, lsem.at[14])
    wo_in.start()

    barrier = pltpu.get_barrier_semaphore()
    peers = [(sibling, z)]
    for d in STEP:
        peers.append((ctx, (z + d) % N))
        for core in range(2):
            peers.append((cid(y, (x + d) % N, core), z))
            peers.append((cid((y + d) % N, x, core), z))
    for peer in peers:
        pl.semaphore_signal(barrier, inc=1, device_id=peer, device_id_type=pl.DeviceIdType.MESH)
    pl.semaphore_wait(barrier, len(peers))

    half_rows = (pl.ds(0, R // 2), pl.ds(R // 2, R // 2))

    def gather_own(h):
        for turn in range(2):
            for way in (RIGHT, LEFT):
                part = way ^ turn
                block = xg.at[h, z, half_rows[part]]
                to = (z + STEP[way]) % N
                send(block, block, gs.at[h, way, part], gr.at[h, way, part], ctx, to)

    def gather_relay(h):
        for way in (RIGHT, LEFT):
            block = xg.at[h, (z + N - STEP[way]) % N, half_rows[way]]
            arrive(block, gr.at[h, way, way])
            send(block, block, gs.at[h, 2, way], gr.at[h, 2, way], ctx, (z + STEP[way]) % N)

    def gather_rest(h, way):
        part = 1 - way
        arrive(xg.at[h, (z + N - STEP[way]) % N, half_rows[part]], gr.at[h, way, part])

    def gather_last(h):
        for way in (RIGHT, LEFT):
            arrive(xg.at[h, (z + 2) % N, half_rows[way]], gr.at[h, 2, way])

    def weights(at):
        for j in range(3):
            w_in[at * 3 + j].wait()

    def project(hs, rel, first):
        src = (z + rel) % N
        rows = pl.ds(pl.multiple_of(src * DW, DW), DW)

        def tile(j, carry):
            at = pl.ds(pl.multiple_of(j * DW, DW), DW)
            w = wq[j, rows, :]
            if len(hs) == 2:
                a = jnp.concatenate([xg[h, src] for h in hs], axis=0)
            else:
                a = xg[hs[0], src]
            part = jnp.dot(a, w, preferred_element_type=F32)
            for n, h in enumerate(hs):
                piece = part[n * R : (n + 1) * R]
                if first:
                    acc[h, :, at] = piece
                else:
                    acc[h, :, at] += piece
            return carry

        lax.fori_loop(0, 3, tile, 0)

    def tables():
        perm_in.wait()
        tab_in.wait()
        for s in range(4):
            at = perm[4 * ctx + s]
            rows = pl.ds(s * WW, WW)
            cost[rows, :] = tab[pl.ds(at, 1), :] + tab[pl.ds(256, WW), :]
            sint[rows, :] = tab[pl.ds(128 + at, 1), :] + tab[pl.ds(256 + WW, WW), :]
        source = lax.broadcasted_iota(jnp.int32, (2 * HD, 2 * HD), 0)
        target = lax.broadcasted_iota(jnp.int32, (2 * HD, 2 * HD), 1)
        lane = target % HD
        distance = jnp.where(lane < 16, 8, 28)
        low = (lane < 8) | ((lane >= 16) & (lane < 44)) | ((lane >= 72) & (lane < 100))
        partner = target + jnp.where(low, distance, -distance)
        swap[...] = jnp.where(source == partner, 1.0, 0.0).astype(BF)

    def finish(h):
        rows = pl.ds(h * R, R)
        cosine, sine = cost[rows, :], sint[rows, :]
        for j in range(2):
            pairs = [acc[h, :, pl.ds(j * DW + i * 2 * HD, 2 * HD)] for i in range(HH)]
            stacked = jnp.concatenate([p.astype(BF) for p in pairs], axis=0)
            other = jnp.dot(stacked, swap[...], preferred_element_type=F32)
            for head in range(2 * HH):
                cols = slice(head % 2 * HD, (head % 2 + 1) * HD)
                v = pairs[head // 2][:, cols]
                w = other[head // 2 * R : (head // 2 + 1) * R, cols]
                square = jnp.mean(v * v, axis=-1, keepdims=True)
                factor = lax.rsqrt(square + EPSILON)
                if j == 0:
                    factor = factor * (HD**-0.5 / math.log(2.0))
                turned = ((v * cosine + w * sine) * factor).astype(BF)
                half, to = head // HH, pl.ds(head % HH * HD, HD)
                if j == 0:
                    oq[half, h, :, to] = turned
                else:
                    okv[half, h, 0, :, to] = turned
        for half in range(2):
            okv[half, h, 1] = acc[h, :, pl.ds(2 * DW + half * HW, HW)].astype(BF)

    def spread(h):
        for turn in range(2):
            for half in range(2):
                kslot, qslot = ((x, y), (y, x))[half]
                for way in (RIGHT, LEFT):
                    part = way ^ turn
                    rows = half_rows[part]
                    send(
                        oq.at[half, h, rows], qb.at[h, qslot, c, rows], qs.at[h, half, way, part],
                        qr.at[h, way, part, c], q_to(half, STEP[way]), z,
                    )
                    send(
                        okv.at[half, h, part], kv.at[h, kslot, c, part], ks.at[h, half, way, part],
                        kr.at[h, way, part, c], kv_to(half, STEP[way]), z,
                    )
        send(oq.at[1 - c, h], qb.at[h, kc, c], sbs.at[h, 0], sbr.at[h, 0], sibling, z)
        send(okv.at[1 - c, h], kv.at[h, qc, c], sbs.at[h, 1], sbr.at[h, 1], sibling, z)
        kv[h, kc, c] = okv[c, h]
        qb[h, qc, c] = oq[c, h]

    def spread_relay(h):
        for way in (RIGHT, LEFT):
            kslot = (kc + N - STEP[way]) % N
            qslot = (qc + N - STEP[way]) % N
            for core in range(2):
                block = qb.at[h, qslot, core, half_rows[way]]
                arrive(block, qr.at[h, way, way, core])
                send(block, block, qrs.at[h, way, core], qrr.at[h, way, core], my_q(STEP[way], c), z)
        for way in (RIGHT, LEFT):
            kslot = (kc + N - STEP[way]) % N
            for core in range(2):
                block = kv.at[h, kslot, core, way]
                arrive(block, kr.at[h, way, way, core])
                send(
                    block, block, krs.at[h, way, core], krr.at[h, way, core], my_kv(STEP[way]), z
                )

    def spread_rest(h):
        arrive(qb.at[h, qc, 1 - c], sbr.at[h, 0])
        arrive(kv.at[h, kc, 1 - c], sbr.at[h, 1])
        for way in (RIGHT, LEFT):
            kslot = (kc + N - STEP[way]) % N
            qslot = (qc + N - STEP[way]) % N
            part = 1 - way
            for core in range(2):
                arrive(qb.at[h, qslot, core, half_rows[part]], qr.at[h, way, part, core])
                arrive(kv.at[h, kslot, core, part], kr.at[h, way, part, core])

    def spread_last_q(h):
        for way in (RIGHT, LEFT):
            for core in range(2):
                arrive(qb.at[h, (qc + 2) % N, core, half_rows[way]], qrr.at[h, way, core])

    def spread_last_kv(h):
        for way in (RIGHT, LEFT):
            for core in range(2):
                arrive(kv.at[h, (kc + 2) % N, core, way], krr.at[h, way, core])

    frame_rows = perm.shape[0] // 8

    def attend(hq, hk, rel, krels, masked, first):
        slot = (qc + rel) % N
        kslots = [(kc + krel) % N for krel in krels]
        if masked:
            fq = [
                perm[4 * cid((1 - c) * slot + c * y, (1 - c) * x + c * slot, a) + 2 * hq] // frame_rows
                for a in range(2)
            ]
            fk = [
                perm[4 * cid((1 - c) * y + c * t, (1 - c) * t + c * x, b) + 2 * hk] // frame_rows
                for t in kslots
                for b in range(2)
            ]
            ok = [[(k <= q).astype(F32) for k in fk] for q in fq]

        for i in range(HH):
            cols = pl.ds(i * HD, HD)
            q = qb[hq, slot, :, :, cols].reshape(2 * R, HD)
            k = jnp.concatenate([kv[hk, t, b, 0, :, cols] for t in kslots for b in range(2)], axis=0)
            v = jnp.concatenate([kv[hk, t, b, 1, :, cols] for t in kslots for b in range(2)], axis=0)
            s = lax.dot_general(q, k, (((1,), (1,)), ((), ())), preferred_element_type=F32)
            w = jnp.exp2(s)
            blocks = range(2 * len(krels))
            if masked:
                w = jnp.concatenate(
                    [
                        jnp.concatenate(
                            [w[a * R : (a + 1) * R, b * R : (b + 1) * R] * ok[a][b] for b in blocks],
                            axis=1,
                        )
                        for a in range(2)
                    ],
                    axis=0,
                )
            total = w[:, :HD]
            for b in blocks[1:]:
                total = total + w[:, b * HD : (b + 1) * HD]
            o = jnp.dot(w.astype(BF), v, preferred_element_type=F32)
            for a in range(2):
                rows = slice(a * R, (a + 1) * R)
                if first:
                    num[hq, slot, a, :, cols] = o[rows]
                    den[hq, slot, a, :, cols] = total[rows]
                else:
                    num[hq, slot, a, :, cols] += o[rows]
                    den[hq, slot, a, :, cols] += total[rows]

    def row_sum(h, slot, core, i):
        return jnp.sum(den[h, slot, core, :, pl.ds(i * HD, HD)].T, axis=0, keepdims=True)

    def pack(dst, h, slot, core, plus=None):
        for i in range(HH):
            cols = pl.ds(i * HD, HD)
            n = num[h, slot, core, :, cols]
            d = row_sum(h, slot, core, i)
            if plus is not None:
                n = n + plus[pl.ds(0, R), cols].astype(F32)
                d = d + plus[pl.ds(R, 8), cols].astype(F32)
            dst[pl.ds(0, R), cols] = n.astype(BF)
            dst[pl.ds(R, 8), cols] = jnp.broadcast_to(d, (8, HD)).astype(BF)

    def sum_far(h):
        far = (qc + 2) % N
        for way in (RIGHT, LEFT):
            pack(os1.at[h, way], h, far, way)
            send(
                os1.at[h, way], or1.at[h, way], o1s.at[h, way], o1r.at[h, way],
                my_q(STEP[way], c), z,
            )

    def sum_near(h, way, core, plus=None):
        pack(os2.at[h, way, core], h, (qc + STEP[way]) % N, core, plus)
        send(
            os2.at[h, way, core], or2.at[h, c, way], o2s.at[h, way, core],
            o2r.at[h, c, way], my_q(STEP[way], core), z,
        )

    def sum_plain(h, way):
        sum_near(h, way, 1 - way)

    def sum_passed(h):
        for way in (RIGHT, LEFT):
            arrive(or1.at[h, way], o1r.at[h, way])
            sum_near(h, way, way, or1.at[h, way])

    def sum_sibling(h):
        pack(oss.at[h], h, qc, 1 - c)
        send(oss.at[h], ors.at[h], oqs.at[h], oqr.at[h], sibling, z)

    def normalize(h):
        for half in range(2):
            for way in (RIGHT, LEFT):
                arrive(or2.at[h, half, way], o2r.at[h, half, way])
        arrive(ors.at[h], oqr.at[h])
        for mine in range(2):
            half = c if mine else 1 - c
            for i in range(HH):
                cols = pl.ds(i * HD, HD)
                if mine:
                    n = num[h, qc, c, :, cols]
                    d = row_sum(h, qc, c, i)
                else:
                    n = ors[h, pl.ds(0, R), cols].astype(F32)
                    d = ors[h, pl.ds(R, 8), cols].astype(F32)[:1]
                for way in (RIGHT, LEFT):
                    n = n + or2[h, half, way, pl.ds(0, R), cols].astype(F32)
                    d = d + or2[h, half, way, pl.ds(R, 8), cols].astype(F32)[:1]
                attn[h, half, :, cols] = (n / jnp.broadcast_to(d, (HD, R)).T).astype(BF)

    def mixed_for(h, rel, store):
        base = (z + rel) % N * DW

        for t in range(3):
            cols = pl.ds(pl.multiple_of(base + t * 256, 256), 256)
            part = jnp.dot(attn[h, 0], wo[pl.ds(0, HW), cols], preferred_element_type=F32)
            part += jnp.dot(attn[h, 1], wo[pl.ds(HW, HW), cols], preferred_element_type=F32)
            store(pl.ds(t * 256, 256), part)

    def mix_far(h):
        def store(cols, part):
            for way in (RIGHT, LEFT):
                zs1[h, way, :, cols] = part[way * (R // 2) : (way + 1) * (R // 2)].astype(BF)

        mixed_for(h, 2, store)
        for way in (RIGHT, LEFT):
            send(
                zs1.at[h, way], zr1.at[h, way], z1s.at[h, way], z1r.at[h, way],
                ctx, (z + STEP[way]) % N,
            )

    def mix_send(h, way, part):
        send(
            zs2.at[h, way, part], zr2.at[h, way, part], z2s.at[h, way, part], z2r.at[h, way, part],
            ctx, (z + STEP[way]) % N,
        )

    def mix_plain(h, way):
        part = 1 - way

        def store(cols, rows):
            zp[h, way, :, cols] = rows[way * (R // 2) : (way + 1) * (R // 2)]
            zs2[h, way, part, :, cols] = rows[part * (R // 2) : (part + 1) * (R // 2)].astype(BF)

        mixed_for(h, STEP[way], store)
        mix_send(h, way, part)

    def mix_own(h):
        def store(cols, rows):
            own[h, :, cols] = rows

        mixed_for(h, 0, store)

    def mix_passed(h):
        for way in (RIGHT, LEFT):
            arrive(zr1.at[h, way], z1r.at[h, way])
            zs2[h, way, way] = (zp[h, way] + zr1[h, way].astype(F32)).astype(BF)
            mix_send(h, way, way)

    def mix_last(h):
        for part in (1, 0):
            total = own[h, half_rows[part], :]
            for way in ((RIGHT, LEFT) if part else (LEFT, RIGHT)):
                arrive(zr2.at[h, way, part], z2r.at[h, way, part])
                total = total + zr2[h, way, part].astype(F32)
            mixed[h, half_rows[part], :] = total.astype(BF)
        copy = pltpu.make_async_copy(mixed.at[h], out.at[pl.ds(h * R, R)], lsem.at[h])
        copy.start()
        outgoing.append(copy)

    near = (1, 3, 0)
    every = (1, 3, 0, 2)
    outgoing = []
    tok_in[0].wait()
    gather_own(0)
    tables()
    tok_in[1].wait()
    weights(0)
    project((0, 1), 0, True)
    gather_relay(0)
    gather_own(1)
    weights(1)
    gather_rest(0, RIGHT)
    project((0,), 3, False)
    weights(2)
    gather_rest(0, LEFT)
    project((0,), 1, False)
    weights(3)
    gather_last(0)
    project((0,), 2, False)
    finish(0)
    spread(0)
    gather_relay(1)
    gather_rest(1, RIGHT)
    project((1,), 3, False)
    gather_rest(1, LEFT)
    project((1,), 1, False)
    spread_relay(0)
    gather_last(1)
    project((1,), 2, False)
    finish(1)
    spread(1)
    spread_rest(0)
    spread_last_q(0)
    spread_last_kv(0)
    attend(0, 0, 2, every, True, True)
    attend(0, 0, 1, every, True, True)
    spread_relay(1)
    sum_far(0)
    attend(0, 0, 3, every, True, True)
    attend(0, 0, 0, every, True, True)
    spread_rest(1)
    attend(1, 0, 1, every, False, True)
    sum_plain(0, RIGHT)
    sum_plain(0, LEFT)
    sum_sibling(0)
    attend(1, 0, 3, every, False, True)
    sum_passed(0)
    attend(1, 0, 0, every, False, True)
    attend(1, 1, 1, near, True, False)
    attend(1, 1, 3, near, True, False)
    attend(1, 1, 0, near, True, False)
    spread_last_q(1)
    attend(1, 0, 2, every, False, True)
    spread_last_kv(1)
    attend(1, 1, 2, every, True, False)
    sum_far(1)
    attend(1, 1, 1, (2,), True, False)
    sum_plain(1, RIGHT)
    attend(1, 1, 3, (2,), True, False)
    sum_plain(1, LEFT)
    attend(1, 1, 0, (2,), True, False)
    sum_sibling(1)
    wo_in.wait()
    normalize(0)
    mix_far(0)
    mix_plain(0, RIGHT)
    sum_passed(1)
    mix_plain(0, LEFT)
    mix_own(0)
    mix_passed(0)
    normalize(1)
    mix_far(1)
    mix_plain(1, RIGHT)
    mix_plain(1, LEFT)
    mix_own(1)
    mix_last(0)
    mix_passed(1)
    mix_last(1)
    for copy in outgoing:
        copy.wait()
    for copy in pending:
        copy.wait_send()


def per_device(tokens, w_qkv, w_out, block_perm):
    table = jnp.asarray(np.concatenate(rope_tables(block_perm.shape[0] // 8)))
    hbm = pl.BlockSpec(memory_space=pl.ANY)
    dma = pltpu.SemaphoreType.DMA
    return pl.pallas_call(
        kernel,
        name="attention_layer",
        out_shape=jax.ShapeDtypeStruct((2 * R, DW), BF),
        in_specs=[hbm] * 5,
        out_specs=hbm,
        scratch_shapes=[
            pltpu.SMEM(block_perm.shape, jnp.int32),
            pltpu.VMEM(table.shape, F32),
            pltpu.VMEM((2, N, R, DW), BF),
            pltpu.VMEM((3, N * DW, DW), BF),
            pltpu.VMEM((DW, N * DW), BF),
            pltpu.VMEM((2, R, 3 * DW), F32),
            pltpu.VMEM((2 * R, HD), F32),
            pltpu.VMEM((2 * R, HD), F32),
            pltpu.VMEM((2 * HD, 2 * HD), BF),
            pltpu.VMEM((2, 2, 2, R, HW), BF),
            pltpu.VMEM((2, 2, R, HW), BF),
            pltpu.VMEM((2, N, 2, 2, R, HW), BF),
            pltpu.VMEM((2, N, 2, R, HW), BF),
            pltpu.VMEM((2, N, 2, R, HW), F32),
            pltpu.VMEM((2, N, 2, R, HW), F32),
            pltpu.VMEM((2, 2, OB, HW), BF),
            pltpu.VMEM((2, 2, OB, HW), BF),
            pltpu.VMEM((2, 2, 2, OB, HW), BF),
            pltpu.VMEM((2, 2, 2, OB, HW), BF),
            pltpu.VMEM((2, OB, HW), BF),
            pltpu.VMEM((2, OB, HW), BF),
            pltpu.VMEM((2, 2, R, HW), BF),
            pltpu.VMEM((2, 2, R // 2, DW), BF),
            pltpu.VMEM((2, 2, R // 2, DW), BF),
            pltpu.VMEM((2, 2, R // 2, DW), F32),
            pltpu.VMEM((2, R, DW), F32),
            pltpu.VMEM((2, 2, 2, R // 2, DW), BF),
            pltpu.VMEM((2, 2, 2, R // 2, DW), BF),
            pltpu.VMEM((2, R, DW), BF),
            dma((17,)),
            dma((2, 3, 2)),
            dma((2, 3, 2)),
            dma((2, 2, 2, 2)),
            dma((2, 2, 2, 2)),
            dma((2, 2, 2)),
            dma((2, 2, 2)),
            dma((2, 2, 2, 2)),
            dma((2, 2, 2, 2)),
            dma((2, 2, 2)),
            dma((2, 2, 2)),
            dma((2, 2)),
            dma((2, 2)),
            dma((2, 2)),
            dma((2, 2)),
            dma((2, 2, 2)),
            dma((2, 2, 2)),
            dma((2,)),
            dma((2,)),
            dma((2, 2)),
            dma((2, 2)),
            dma((2, 2, 2)),
            dma((2, 2, 2)),
        ],
        compiler_params=pltpu.CompilerParams(
            collective_id=0, has_side_effects=True, vmem_limit_bytes=64 * 1024 * 1024 - 65536
        ),
    )(block_perm, table, tokens, w_qkv, w_out)


def solution(mesh):
    in_specs = (P("ctx", "head"), P(None, None, "head"), P("head", None), P())
    return jax.shard_map(
        per_device, mesh=mesh, in_specs=in_specs, out_specs=P("ctx", "head"), check_vma=False
    )
```

time: 78.5 us -> 66.4 us (0.85)
  Pallas kernels: 75.9 us -> 64.5 us
    pallas_call x1, Pallas kernels: 75.9 us -> 64.5 us  [per_device(): pl.pallas_call(kernel, name='attention_layer', out_shape=jax.ShapeDtypeSt...]
where the time goes in v2:
time: 66.4 us; the launch traced here: 66.2 us
  Pallas kernels  64.5 us (97%)
  local copies, waits for them, and re-layouts  1.77 us (3%)
    pallas_call x1, Pallas kernels, per_device(): pl.pallas_call(kernel, name='attention_layer', out_shape=jax.ShapeDtypeSt...  64.5 us
    unnamed x1, local copies, waits for them, and re-layouts  1.77 us

profile of v2, /device:TPU:0, one launch (start us, length us, event | category | flops | bytes accessed | tf_op | source)
XLA Modules:
  0.0 66.2 jit_solution(943446795278904181)
XLA Ops:
  0.0 64.5 %attention_layer.1 = bf16[256,768]{1,0:T(8,128)(2,1)} custom-call(s32[128]{0:T(128)} %perm_hbm.1, f32[384,128]{1,0:T(8,128)} %constant.2.clone.tab_hbm, bf16[256,768]{1,0:T(8,128)(2,1)} %tok.1, bf16[3,3072,768]{2,1,0:T(8,128)(2,1)} %wqkv.1, bf16[768,3072]{1,0:T(8,128)(2,1)} %wout.1), custom_call_target="tpu_custom_call" | custom-call | tf_op jit(solution)/shard_map/attention_layer/pallas_call | solution.py:540
  64.5 1.8 %copy.7 = bf16[256,768]{1,0:T(8,128)(2,1)} copy(bf16[256,768]{1,0:T(8,128)(2,1)} %attention_layer.1) | data formatting | bytes 786432

commit v3 on v2

v3 whole, which is shorter than its diff:
```python
import functools
import math

import jax
import jax.numpy as jnp
import numpy as np
from jax import lax
from jax.experimental import pallas as pl
from jax.experimental.pallas import tpu as pltpu
from jax.sharding import PartitionSpec as P

HD = 128
WW = 64
ROPE_BASE = 10000.0
EPSILON = 1e-06
N = 4
R = 128
HH = 3
HW = HH * HD
DW = 2 * HW
OB = R + 8
BF = jnp.bfloat16
F32 = jnp.float32
RIGHT, LEFT = 0, 1
EARLY, LATE = 0, 1
C0, C1, C2 = (EARLY, 0, R // 2, 0), (EARLY, R // 2, R // 2, 1), (LATE, 0, R, 2)
STEP = (1, N - 1)


def rope_tables(frame_rows):
    parts = ((0, HD // 16), (HD // 8, 7 * HD // 32), (HD // 8 + 7 * HD // 16, 7 * HD // 32))
    frames = np.arange(128) // frame_rows
    rows = np.arange(128) % frame_rows
    tables = []
    for position, kinds in ((np.stack([frames, rows]), (0, 1)), (np.arange(WW)[None], (2,))):
        cosine = np.zeros((position.shape[1], HD), np.float32)
        sine = np.zeros((position.shape[1], HD), np.float32)
        for at, kind in enumerate(kinds):
            first, pairs = parts[kind]
            freq = np.float32(ROPE_BASE) ** (-np.arange(pairs, dtype=np.float32) / pairs)
            angle = position[at].astype(np.float32)[:, None] * freq[None, :].astype(np.float32)
            cosine[:, first : first + pairs] = np.cos(angle)
            cosine[:, first + pairs : first + 2 * pairs] = np.cos(angle)
            sine[:, first : first + pairs] = -np.sin(angle)
            sine[:, first + pairs : first + 2 * pairs] = np.sin(angle)
        tables += [cosine, sine]
    return tables


def kernel(
    perm_hbm, tab_hbm, tok, wqkv, wout, out,
    perm, tab, xg, wq, wo, acc, cost, sint, swap, okv, oq, kv, qb, num, den,
    os1, or1, os2, or2, oss, ors, attn, zs1, zr1, zp, own, zs2, zr2, mixed,
    lsem, gs, gr, xs, xr, o1s, o1r, o2s, o2r, oqs, oqr, z1s, z1r, z2s, z2r,
):
    ctx = lax.axis_index("ctx")
    z = lax.axis_index("head")
    c = ctx % 2
    x = (ctx // 2) % N
    y = ctx // (2 * N)

    def cid(yy, xx, cc):
        return (yy * N + xx) * 2 + cc

    def kv_to(half, d):
        if half == 0:
            return cid(y, (x + d) % N, 0)
        return cid((y + d) % N, x, 1)

    def q_to(half, d):
        if half == 0:
            return cid((y + d) % N, x, 0)
        return cid(y, (x + d) % N, 1)

    def my_kv(d):
        return cid((y + c * d) % N, (x + (1 - c) * d) % N, c)

    def my_q(d, core):
        return cid((y + (1 - c) * d) % N, (x + c * d) % N, core)

    sibling = cid(y, x, 1 - c)
    kc = x * (1 - c) + y * c
    qc = y * (1 - c) + x * c

    def send(src, dst, ss, rs, to_ctx, to_z):
        pltpu.make_async_remote_copy(
            src_ref=src, dst_ref=dst, send_sem=ss, recv_sem=rs,
            device_id=(to_ctx, to_z), device_id_type=pl.DeviceIdType.MESH,
        ).start()

    def sized(ref, sem):
        return pltpu.make_async_remote_copy(
            src_ref=ref, dst_ref=ref, send_sem=sem, recv_sem=sem,
            device_id=(sibling, z), device_id_type=pl.DeviceIdType.MESH,
        )

    def arrive(dst, rs):
        sized(dst, rs).wait_recv()

    def left_here(src, ss):
        sized(src, ss).wait_send()

    perm_in = pltpu.make_async_copy(perm_hbm, perm, lsem.at[7])
    perm_in.start()
    tab_in = pltpu.make_async_copy(tab_hbm, tab, lsem.at[8])
    tab_in.start()
    tok_in = [
        pltpu.make_async_copy(tok.at[pl.ds(h * R, R)], xg.at[h, z], lsem.at[h]) for h in range(2)
    ]
    for copy in tok_in:
        copy.start()
    w_in = []
    for at, rel in enumerate((0, 3, 1, 2)):
        rows = pl.ds(pl.multiple_of((z + rel) % N * DW, DW), DW)
        w_in.append(pltpu.make_async_copy(wqkv.at[:, rows], wq.at[:, rows], lsem.at[2 + at]))
    for copy in w_in:
        copy.start()
    wo_in = pltpu.make_async_copy(wout, wo, lsem.at[6])
    wo_in.start()

    barrier = pltpu.get_barrier_semaphore()
    peers = [(sibling, z)]
    for d in STEP:
        peers.append((ctx, (z + d) % N))
        for core in range(2):
            peers.append((cid(y, (x + d) % N, core), z))
            peers.append((cid((y + d) % N, x, core), z))
    for peer in peers:
        pl.semaphore_signal(barrier, inc=1, device_id=peer, device_id_type=pl.DeviceIdType.MESH)
    pl.semaphore_wait(barrier, len(peers))

    half_rows = (pl.ds(0, R // 2), pl.ds(R // 2, R // 2))

    def halves(chunk):
        h, first, count, at = chunk
        return pl.ds(first, count // 2), pl.ds(first + count // 2, count // 2)

    def gather_own(chunk, turn):
        h, _, _, at = chunk
        for way in (RIGHT, LEFT):
            block = xg.at[h, z, halves(chunk)[way ^ turn]]
            got = gr.at[at, 1 + way if turn else 0]
            send(block, block, gs.at[at], got, ctx, (z + STEP[way]) % N)

    def gather_relay(chunk):
        h, first, count, at = chunk
        arrive(xg.at[h, z, pl.ds(first, count)], gr.at[at, 0])
        for way in (RIGHT, LEFT):
            block = xg.at[h, (z + N - STEP[way]) % N, halves(chunk)[way]]
            send(block, block, gs.at[at], gr.at[at, 3], ctx, (z + STEP[way]) % N)

    def gather_rest(chunk, way):
        h, _, _, at = chunk
        arrive(xg.at[h, (z + N - STEP[way]) % N, halves(chunk)[1 - way]], gr.at[at, 1 + way])

    def gather_last(chunk):
        h, first, count, at = chunk
        arrive(xg.at[h, (z + 2) % N, pl.ds(first, count)], gr.at[at, 3])

    def weights(at):
        w_in[at].wait()

    def project_own():
        rows = pl.ds(pl.multiple_of(z * DW, DW), DW)

        def tile(j, carry):
            at = pl.ds(pl.multiple_of(j * DW, DW), DW)
            a = jnp.concatenate([xg[h, z] for h in range(2)], axis=0)
            part = jnp.dot(a, wq[j, rows, :], preferred_element_type=F32)
            for h in range(2):
                acc[h, :, at] = part[h * R : (h + 1) * R]
            return carry

        lax.fori_loop(0, 3, tile, 0)

    def project(chunk, rel):
        h, first, count, _ = chunk
        src = (z + rel) % N
        rows = pl.ds(pl.multiple_of(src * DW, DW), DW)
        mine = pl.ds(first, count)

        def tile(j, carry):
            at = pl.ds(pl.multiple_of(j * DW, DW), DW)
            acc[h, mine, at] += jnp.dot(
                xg[h, src, mine], wq[j, rows, :], preferred_element_type=F32
            )
            return carry

        lax.fori_loop(0, 3, tile, 0)

    def tables():
        perm_in.wait()
        tab_in.wait()
        for s in range(4):
            at = perm[4 * ctx + s]
            rows = pl.ds(s * WW, WW)
            cost[rows, :] = tab[pl.ds(at, 1), :] + tab[pl.ds(256, WW), :]
            sint[rows, :] = tab[pl.ds(128 + at, 1), :] + tab[pl.ds(256 + WW, WW), :]
        source = lax.broadcasted_iota(jnp.int32, (2 * HD, 2 * HD), 0)
        target = lax.broadcasted_iota(jnp.int32, (2 * HD, 2 * HD), 1)
        lane = target % HD
        distance = jnp.where(lane < 16, 8, 28)
        low = (lane < 8) | ((lane >= 16) & (lane < 44)) | ((lane >= 72) & (lane < 100))
        partner = target + jnp.where(low, distance, -distance)
        swap[...] = jnp.where(source == partner, 1.0, 0.0).astype(BF)

    def finish(chunk):
        h, first, count, _ = chunk
        mine = pl.ds(first, count)
        cosine = cost[pl.ds(h * R + first, count), :]
        sine = sint[pl.ds(h * R + first, count), :]
        for j in range(2):
            pairs = [acc[h, mine, pl.ds(j * DW + i * 2 * HD, 2 * HD)] for i in range(HH)]
            stacked = jnp.concatenate([p.astype(BF) for p in pairs], axis=0)
            other = jnp.dot(stacked, swap[...], preferred_element_type=F32)
            for head in range(2 * HH):
                cols = slice(head % 2 * HD, (head % 2 + 1) * HD)
                v = pairs[head // 2][:, cols]
                w = other[head // 2 * count : (head // 2 + 1) * count, cols]
                square = jnp.mean(v * v, axis=-1, keepdims=True)
                factor = lax.rsqrt(square + EPSILON)
                if j == 0:
                    factor = factor * (HD**-0.5 / math.log(2.0))
                turned = ((v * cosine + w * sine) * factor).astype(BF)
                half, to = head // HH, pl.ds(head % HH * HD, HD)
                if j == 0:
                    oq[half, h, mine, to] = turned
                else:
                    okv[half, h, 0, mine, to] = turned
        for half in range(2):
            okv[half, h, 1, mine] = acc[h, mine, pl.ds(2 * DW + half * HW, HW)].astype(BF)

    def spread(chunk):
        h, first, count, at = chunk
        rows = pl.ds(first, count)
        for turn in range(2):
            for half in range(2):
                qslot = (y, x)[half]
                for way in (RIGHT, LEFT):
                    part = halves(chunk)[way ^ turn]
                    src, dst = oq.at[half, h, part], qb.at[h, qslot, c, part]
                    send(src, dst, xs.at[at, 0], xr.at[at, turn], q_to(half, STEP[way]), z)
        send(
            oq.at[1 - c, h, rows], qb.at[h, kc, c, rows], xs.at[at, 2], xr.at[at, 2], sibling, z
        )
        qb[h, qc, c, rows] = oq[c, h, rows]
        for turn in range(2):
            for half in range(2):
                kslot = (x, y)[half]
                for way in (RIGHT, LEFT):
                    part = way ^ turn
                    src, dst = okv.at[half, h, part, rows], kv.at[h, kslot, c, part, rows]
                    send(src, dst, xs.at[at, 0], xr.at[at, 4 + turn], kv_to(half, STEP[way]), z)
        send(
            okv.at[1 - c, h, :, rows], kv.at[h, qc, c, :, rows],
            xs.at[at, 3], xr.at[at, 6], sibling, z,
        )
        kv[h, kc, c, :, rows] = okv[c, h, :, rows]

    def spread_relay_q(chunk):
        h, first, count, at = chunk
        arrive(qb.at[h, qc, :, pl.ds(first, count)], xr.at[at, 0])
        for way in (RIGHT, LEFT):
            for core in range(2):
                block = qb.at[h, (qc + N - STEP[way]) % N, core, halves(chunk)[way]]
                send(block, block, xs.at[at, 1], xr.at[at, 3], my_q(STEP[way], c), z)

    def spread_relay_kv(chunk):
        h, first, count, at = chunk
        arrive(kv.at[h, kc, :, :, pl.ds(first, count)], xr.at[at, 4])
        for way in (RIGHT, LEFT):
            for core in range(2):
                block = kv.at[h, (kc + N - STEP[way]) % N, core, way, pl.ds(first, count)]
                send(block, block, xs.at[at, 1], xr.at[at, 7], my_kv(STEP[way]), z)

    def spread_sibling_q(chunk):
        h, first, count, at = chunk
        arrive(qb.at[h, qc, 1 - c, pl.ds(first, count)], xr.at[at, 2])

    def spread_rest_q(chunk):
        h, first, count, at = chunk
        arrive(qb.at[h, qc, :, pl.ds(first, count)], xr.at[at, 1])

    def spread_rest_kv(chunk):
        h, first, count, at = chunk
        arrive(kv.at[h, kc, 1 - c, :, pl.ds(first, count)], xr.at[at, 6])
        arrive(kv.at[h, kc, :, :, pl.ds(first, count)], xr.at[at, 5])

    def spread_last_q(chunk):
        h, first, count, at = chunk
        arrive(qb.at[h, (qc + 2) % N, :, pl.ds(first, count)], xr.at[at, 3])

    def spread_last_kv(chunk):
        h, first, count, at = chunk
        arrive(kv.at[h, (kc + 2) % N, :, :, pl.ds(first, count)], xr.at[at, 7])

    frame_rows = perm.shape[0] // 8

    def attend(queries, against):
        rows = [(h, (qc + rel) % N, a, first) for h, rel, first in queries for a in range(2)]
        keys = [(h, (kc + rel) % N, b) for h, rel in against for b in range(2)]
        fq = [
            perm[4 * cid((1 - c) * t + c * y, (1 - c) * x + c * t, a) + 2 * h] // frame_rows
            for h, t, a, _ in rows
        ]
        fk = [
            perm[4 * cid((1 - c) * y + c * t, (1 - c) * t + c * x, b) + 2 * h] // frame_rows
            for h, t, b in keys
        ]

        def seen(w, n, m):
            block = w[n * R : (n + 1) * R, m * R : (m + 1) * R]
            return block * (fk[m] <= fq[n]).astype(F32) if rows[n][0] == keys[m][0] else block

        for i in range(HH):
            cols = pl.ds(i * HD, HD)
            q = jnp.concatenate([qb[h, t, a, :, cols] for h, t, a, _ in rows], axis=0)
            k = jnp.concatenate([kv[h, t, b, 0, :, cols] for h, t, b in keys], axis=0)
            v = jnp.concatenate([kv[h, t, b, 1, :, cols] for h, t, b in keys], axis=0)
            s = lax.dot_general(q, k, (((1,), (1,)), ((), ())), preferred_element_type=F32)
            w = jnp.exp2(s)
            w = jnp.concatenate(
                [
                    jnp.concatenate([seen(w, n, m) for m in range(len(keys))], axis=1)
                    for n in range(len(rows))
                ],
                axis=0,
            )
            total = w[:, :HD]
            for b in range(1, len(keys)):
                total = total + w[:, b * HD : (b + 1) * HD]
            o = jnp.dot(w.astype(BF), v, preferred_element_type=F32)
            for n, (h, t, a, first) in enumerate(rows):
                piece = slice(n * R, (n + 1) * R)
                if first:
                    num[h, t, a, :, cols] = o[piece]
                    den[h, t, a, :, cols] = total[piece]
                else:
                    num[h, t, a, :, cols] += o[piece]
                    den[h, t, a, :, cols] += total[piece]

    def row_sum(h, slot, core, i):
        return jnp.sum(den[h, slot, core, :, pl.ds(i * HD, HD)].T, axis=0, keepdims=True)

    def pack(dst, h, slot, core, plus=None):
        for i in range(HH):
            cols = pl.ds(i * HD, HD)
            n = num[h, slot, core, :, cols]
            d = row_sum(h, slot, core, i)
            if plus is not None:
                n = n + plus[pl.ds(0, R), cols].astype(F32)
                d = d + plus[pl.ds(R, 8), cols].astype(F32)
            dst[pl.ds(0, R), cols] = n.astype(BF)
            dst[pl.ds(R, 8), cols] = jnp.broadcast_to(d, (8, HD)).astype(BF)

    def sum_far(h):
        far = (qc + 2) % N
        for way in (RIGHT, LEFT):
            pack(os1.at[h, way], h, far, way)
            send(os1.at[h, way], or1.at[h, way], o1s.at[h], o1r.at[h], my_q(STEP[way], c), z)

    def sum_near(h, way, core, plus=None):
        pack(os2.at[h, way, core], h, (qc + STEP[way]) % N, core, plus)
        dst = or2.at[h, c, way]
        send(os2.at[h, way, core], dst, o2s.at[h], o2r.at[h], my_q(STEP[way], core), z)

    def sum_plain(h, way):
        sum_near(h, way, 1 - way)

    def sum_passed(h):
        arrive(or1.at[h], o1r.at[h])
        for way in (RIGHT, LEFT):
            sum_near(h, way, way, or1.at[h, way])

    def sum_sibling(h):
        pack(oss.at[h], h, qc, 1 - c)
        send(oss.at[h], ors.at[h], oqs.at[h], oqr.at[h], sibling, z)

    def normalize(h):
        arrive(or2.at[h], o2r.at[h])
        arrive(ors.at[h], oqr.at[h])
        for mine in range(2):
            half = c if mine else 1 - c
            for i in range(HH):
                cols = pl.ds(i * HD, HD)
                if mine:
                    n = num[h, qc, c, :, cols]
                    d = row_sum(h, qc, c, i)
                else:
                    n = ors[h, pl.ds(0, R), cols].astype(F32)
                    d = ors[h, pl.ds(R, 8), cols].astype(F32)[:1]
                for way in (RIGHT, LEFT):
                    n = n + or2[h, half, way, pl.ds(0, R), cols].astype(F32)
                    d = d + or2[h, half, way, pl.ds(R, 8), cols].astype(F32)[:1]
                attn[h, half, :, cols] = (n / jnp.broadcast_to(d, (HD, R)).T).astype(BF)

    def mixed_for(h, rel, store):
        base = (z + rel) % N * DW

        for t in range(3):
            cols = pl.ds(pl.multiple_of(base + t * 256, 256), 256)
            part = jnp.dot(attn[h, 0], wo[pl.ds(0, HW), cols], preferred_element_type=F32)
            part += jnp.dot(attn[h, 1], wo[pl.ds(HW, HW), cols], preferred_element_type=F32)
            store(pl.ds(t * 256, 256), part)

    def mix_far(h):
        def store(cols, part):
            for way in (RIGHT, LEFT):
                zs1[h, way, :, cols] = part[way * (R // 2) : (way + 1) * (R // 2)].astype(BF)

        mixed_for(h, 2, store)
        for way in (RIGHT, LEFT):
            send(zs1.at[h, way], zr1.at[h, way], z1s.at[h], z1r.at[h], ctx, (z + STEP[way]) % N)

    def mix_send(h, way, part):
        src, dst = zs2.at[h, way, part], zr2.at[h, way, part]
        send(src, dst, z2s.at[h], z2r.at[h], ctx, (z + STEP[way]) % N)

    def mix_plain(h, way):
        part = 1 - way

        def store(cols, rows):
            zp[h, way, :, cols] = rows[way * (R // 2) : (way + 1) * (R // 2)]
            zs2[h, way, part, :, cols] = rows[part * (R // 2) : (part + 1) * (R // 2)].astype(BF)

        mixed_for(h, STEP[way], store)
        mix_send(h, way, part)

    def mix_own(h):
        def store(cols, rows):
            own[h, :, cols] = rows

        mixed_for(h, 0, store)

    def mix_passed(h):
        arrive(zr1.at[h], z1r.at[h])
        for way in (RIGHT, LEFT):
            zs2[h, way, way] = (zp[h, way] + zr1[h, way].astype(F32)).astype(BF)
            mix_send(h, way, way)

    def mix_last(h):
        arrive(zr2.at[h], z2r.at[h])
        for part in range(2):
            total = own[h, half_rows[part], :]
            for way in (RIGHT, LEFT):
                total = total + zr2[h, way, part].astype(F32)
            mixed[h, half_rows[part], :] = total.astype(BF)
        copy = pltpu.make_async_copy(mixed.at[h], out.at[pl.ds(h * R, R)], lsem.at[h])
        copy.start()
        outgoing.append(copy)

    near = (1, 3, 0)
    early = [(EARLY, rel) for rel in (1, 3, 0, 2)]
    late = [(LATE, rel) for rel in (1, 3, 0, 2)]
    outgoing = []
    tok_in[0].wait()
    gather_own(C0, 0)
    gather_own(C0, 1)
    gather_own(C1, 0)
    tables()
    tok_in[1].wait()
    weights(0)
    project_own()
    gather_relay(C0)
    gather_own(C1, 1)
    weights(1)
    gather_rest(C0, RIGHT)
    project(C0, 3)
    gather_relay(C1)
    gather_own(C2, 0)
    gather_own(C2, 1)
    weights(2)
    gather_rest(C0, LEFT)
    project(C0, 1)
    weights(3)
    gather_last(C0)
    project(C0, 2)
    finish(C0)
    spread(C0)
    gather_rest(C1, RIGHT)
    project(C1, 3)
    gather_rest(C1, LEFT)
    project(C1, 1)
    gather_last(C1)
    project(C1, 2)
    gather_relay(C2)
    finish(C1)
    spread(C1)
    spread_relay_q(C0)
    spread_relay_kv(C0)
    gather_rest(C2, RIGHT)
    project(C2, 3)
    gather_rest(C2, LEFT)
    project(C2, 1)
    gather_last(C2)
    project(C2, 2)
    finish(C2)
    spread_relay_q(C1)
    spread_relay_kv(C1)
    spread(C2)
    spread_sibling_q(C0)
    spread_sibling_q(C1)
    spread_rest_q(C0)
    spread_rest_q(C1)
    spread_rest_kv(C0)
    spread_rest_kv(C1)
    attend([(EARLY, rel, True) for rel in near], early[:3])
    spread_sibling_q(C2)
    spread_last_q(C0)
    spread_last_q(C1)
    attend([(EARLY, 2, True), (LATE, 0, True)], early[:3])
    spread_relay_q(C2)
    spread_last_kv(C0)
    spread_last_kv(C1)
    attend([(EARLY, rel, False) for rel in (1, 3, 0, 2)] + [(LATE, 0, False)], early[3:])
    sum_far(0)
    spread_rest_q(C2)
    attend([(LATE, 1, True), (LATE, 3, True)], early)
    spread_relay_kv(C2)
    sum_plain(0, RIGHT)
    sum_plain(0, LEFT)
    sum_sibling(0)
    spread_rest_kv(C2)
    attend([(LATE, rel, False) for rel in near], late[:3])
    sum_passed(0)
    spread_last_q(C2)
    attend([(LATE, 2, True)], early + late[:3])
    spread_last_kv(C2)
    attend([(LATE, 2, False)], late[3:])
    sum_far(1)
    attend([(LATE, rel, False) for rel in near], late[3:])
    sum_plain(1, RIGHT)
    sum_plain(1, LEFT)
    sum_sibling(1)
    wo_in.wait()
    normalize(0)
    mix_far(0)
    mix_plain(0, RIGHT)
    mix_plain(0, LEFT)
    sum_passed(1)
    mix_own(0)
    mix_passed(0)
    normalize(1)
    mix_far(1)
    mix_plain(1, RIGHT)
    mix_plain(1, LEFT)
    mix_own(1)
    mix_last(0)
    mix_passed(1)
    mix_last(1)
    for h, first, count, at in (C0, C1, C2):
        rows = pl.ds(first, count)
        left_here(xg.at[h, pl.ds(0, 3), rows], gs.at[at])
        left_here(kv.at[h, pl.ds(0, 3), :, :, rows], xs.at[at, 0])
        left_here(qb.at[h, pl.ds(0, 3), :, rows], xs.at[at, 1])
        left_here(oq.at[1 - c, h, rows], xs.at[at, 2])
        left_here(okv.at[1 - c, h, :, rows], xs.at[at, 3])
    for h in range(2):
        left_here(os1.at[h], o1s.at[h])
        left_here(os2.at[h], o2s.at[h])
        left_here(oss.at[h], oqs.at[h])
        left_here(zs1.at[h], z1s.at[h])
        left_here(zs2.at[h], z2s.at[h])
    for copy in outgoing:
        copy.wait()


def per_device(tokens, w_qkv, w_out, block_perm):
    table = jnp.asarray(np.concatenate(rope_tables(block_perm.shape[0] // 8)))
    hbm = pl.BlockSpec(memory_space=pl.ANY)
    dma = pltpu.SemaphoreType.DMA
    return pl.pallas_call(
        kernel,
        name="attention_layer",
        out_shape=jax.ShapeDtypeStruct((2 * R, DW), BF),
        in_specs=[hbm] * 5,
        out_specs=hbm,
        scratch_shapes=[
            pltpu.SMEM(block_perm.shape, jnp.int32),
            pltpu.VMEM(table.shape, F32),
            pltpu.VMEM((2, N, R, DW), BF),
            pltpu.VMEM((3, N * DW, DW), BF),
            pltpu.VMEM((DW, N * DW), BF),
            pltpu.VMEM((2, R, 3 * DW), F32),
            pltpu.VMEM((2 * R, HD), F32),
            pltpu.VMEM((2 * R, HD), F32),
            pltpu.VMEM((2 * HD, 2 * HD), BF),
            pltpu.VMEM((2, 2, 2, R, HW), BF),
            pltpu.VMEM((2, 2, R, HW), BF),
            pltpu.VMEM((2, N, 2, 2, R, HW), BF),
            pltpu.VMEM((2, N, 2, R, HW), BF),
            pltpu.VMEM((2, N, 2, R, HW), F32),
            pltpu.VMEM((2, N, 2, R, HW), F32),
            pltpu.VMEM((2, 2, OB, HW), BF),
            pltpu.VMEM((2, 2, OB, HW), BF),
            pltpu.VMEM((2, 2, 2, OB, HW), BF),
            pltpu.VMEM((2, 2, 2, OB, HW), BF),
            pltpu.VMEM((2, OB, HW), BF),
            pltpu.VMEM((2, OB, HW), BF),
            pltpu.VMEM((2, 2, R, HW), BF),
            pltpu.VMEM((2, 2, R // 2, DW), BF),
            pltpu.VMEM((2, 2, R // 2, DW), BF),
            pltpu.VMEM((2, 2, R // 2, DW), F32),
            pltpu.VMEM((2, R, DW), F32),
            pltpu.VMEM((2, 2, 2, R // 2, DW), BF),
            pltpu.VMEM((2, 2, 2, R // 2, DW), BF),
            pltpu.VMEM((2, R, DW), BF),
            dma((9,)),
            dma((3,)),
            dma((3, 4)),
            dma((3, 4)),
            dma((3, 8)),
            dma((2,)),
            dma((2,)),
            dma((2,)),
            dma((2,)),
            dma((2,)),
            dma((2,)),
            dma((2,)),
            dma((2,)),
            dma((2,)),
            dma((2,)),
        ],
        compiler_params=pltpu.CompilerParams(
            collective_id=0, has_side_effects=True, vmem_limit_bytes=64 * 1024 * 1024 - 65536
        ),
    )(block_perm, table, tokens, w_qkv, w_out)


def solution(mesh):
    in_specs = (P("ctx", "head"), P(None, None, "head"), P("head", None), P())
    return jax.shard_map(
        per_device, mesh=mesh, in_specs=in_specs, out_specs=P("ctx", "head"), check_vma=False
    )
```

time: 66.4 us -> 64.1 us (0.965)
  Pallas kernels: 64.5 us -> 62.2 us
    pallas_call x1, Pallas kernels: 64.5 us -> 62.2 us  [per_device(): pl.pallas_call(kernel, name='attention_layer', out_shape=jax.ShapeDtypeSt...]
where the time goes in v3:
time: 64.1 us; the launch traced here: 64 us
  Pallas kernels  62.2 us (97%)
  local copies, waits for them, and re-layouts  1.77 us (3%)
    pallas_call x1, Pallas kernels, per_device(): pl.pallas_call(kernel, name='attention_layer', out_shape=jax.ShapeDtypeSt...  62.2 us
    unnamed x1, local copies, waits for them, and re-layouts  1.77 us

profile of v3, /device:TPU:0, one launch (start us, length us, event | category | flops | bytes accessed | tf_op | source)
XLA Modules:
  0.0 64.0 jit_solution(13487632820038157980)
XLA Ops:
  0.0 62.2 %attention_layer.1 = bf16[256,768]{1,0:T(8,128)(2,1)} custom-call(s32[128]{0:T(128)} %perm_hbm.1, f32[384,128]{1,0:T(8,128)} %constant.2.clone.tab_hbm, bf16[256,768]{1,0:T(8,128)(2,1)} %tok.1, bf16[3,3072,768]{2,1,0:T(8,128)(2,1)} %wqkv.1, bf16[768,3072]{1,0:T(8,128)(2,1)} %wout.1), custom_call_target="tpu_custom_call" | custom-call | tf_op jit(solution)/shard_map/attention_layer/pallas_call | solution.py:572
  62.2 1.8 %copy.7 = bf16[256,768]{1,0:T(8,128)(2,1)} copy(bf16[256,768]{1,0:T(8,128)(2,1)} %attention_layer.1) | data formatting | bytes 786432

commit v4 on v3

--- a/solution.py
+++ b/solution.py
@@ -140,14 +140,14 @@
         for way in (RIGHT, LEFT):
             block = xg.at[h, z, halves(chunk)[way ^ turn]]
             got = gr.at[at, 1 + way if turn else 0]
-            send(block, block, gs.at[at], got, ctx, (z + STEP[way]) % N)
+            send(block, block, gs.at[0], got, ctx, (z + STEP[way]) % N)
 
     def gather_relay(chunk):
         h, first, count, at = chunk
         arrive(xg.at[h, z, pl.ds(first, count)], gr.at[at, 0])
         for way in (RIGHT, LEFT):
             block = xg.at[h, (z + N - STEP[way]) % N, halves(chunk)[way]]
-            send(block, block, gs.at[at], gr.at[at, 3], ctx, (z + STEP[way]) % N)
+            send(block, block, gs.at[0], gr.at[at, 3], ctx, (z + STEP[way]) % N)
 
     def gather_rest(chunk, way):
         h, _, _, at = chunk
@@ -239,9 +239,9 @@
                 for way in (RIGHT, LEFT):
                     part = halves(chunk)[way ^ turn]
                     src, dst = oq.at[half, h, part], qb.at[h, qslot, c, part]
-                    send(src, dst, xs.at[at, 0], xr.at[at, turn], q_to(half, STEP[way]), z)
+                    send(src, dst, xs.at[0], xr.at[at, turn], q_to(half, STEP[way]), z)
         send(
-            oq.at[1 - c, h, rows], qb.at[h, kc, c, rows], xs.at[at, 2], xr.at[at, 2], sibling, z
+            oq.at[1 - c, h, rows], qb.at[h, kc, c, rows], xs.at[2], xr.at[at, 2], sibling, z
         )
         qb[h, qc, c, rows] = oq[c, h, rows]
         for turn in range(2):
@@ -250,10 +250,10 @@
                 for way in (RIGHT, LEFT):
                     part = way ^ turn
                     src, dst = okv.at[half, h, part, rows], kv.at[h, kslot, c, part, rows]
-                    send(src, dst, xs.at[at, 0], xr.at[at, 4 + turn], kv_to(half, STEP[way]), z)
+                    send(src, dst, xs.at[0], xr.at[at, 4 + turn], kv_to(half, STEP[way]), z)
         send(
             okv.at[1 - c, h, :, rows], kv.at[h, qc, c, :, rows],
-            xs.at[at, 3], xr.at[at, 6], sibling, z,
+            xs.at[3], xr.at[at, 6], sibling, z,
         )
         kv[h, kc, c, :, rows] = okv[c, h, :, rows]
 
@@ -263,7 +263,7 @@
         for way in (RIGHT, LEFT):
             for core in range(2):
                 block = qb.at[h, (qc + N - STEP[way]) % N, core, halves(chunk)[way]]
-                send(block, block, xs.at[at, 1], xr.at[at, 3], my_q(STEP[way], c), z)
+                send(block, block, xs.at[1], xr.at[at, 3], my_q(STEP[way], c), z)
 
     def spread_relay_kv(chunk):
         h, first, count, at = chunk
@@ -271,7 +271,7 @@
         for way in (RIGHT, LEFT):
             for core in range(2):
                 block = kv.at[h, (kc + N - STEP[way]) % N, core, way, pl.ds(first, count)]
-                send(block, block, xs.at[at, 1], xr.at[at, 7], my_kv(STEP[way]), z)
+                send(block, block, xs.at[1], xr.at[at, 7], my_kv(STEP[way]), z)
 
     def spread_sibling_q(chunk):
         h, first, count, at = chunk
@@ -357,12 +357,12 @@
         far = (qc + 2) % N
         for way in (RIGHT, LEFT):
             pack(os1.at[h, way], h, far, way)
-            send(os1.at[h, way], or1.at[h, way], o1s.at[h], o1r.at[h], my_q(STEP[way], c), z)
+            send(os1.at[h, way], or1.at[h, way], o1s.at[0], o1r.at[h], my_q(STEP[way], c), z)
 
     def sum_near(h, way, core, plus=None):
         pack(os2.at[h, way, core], h, (qc + STEP[way]) % N, core, plus)
         dst = or2.at[h, c, way]
-        send(os2.at[h, way, core], dst, o2s.at[h], o2r.at[h], my_q(STEP[way], core), z)
+        send(os2.at[h, way, core], dst, o2s.at[0], o2r.at[h], my_q(STEP[way], core), z)
 
     def sum_plain(h, way):
         sum_near(h, way, 1 - way)
@@ -374,7 +374,7 @@
 
     def sum_sibling(h):
         pack(oss.at[h], h, qc, 1 - c)
-        send(oss.at[h], ors.at[h], oqs.at[h], oqr.at[h], sibling, z)
+        send(oss.at[h], ors.at[h], oqs.at[0], oqr.at[h], sibling, z)
 
     def normalize(h):
         arrive(or2.at[h], o2r.at[h])
@@ -407,14 +407,14 @@
         def store(cols, part):
             for way in (RIGHT, LEFT):
                 zs1[h, way, :, cols] = part[way * (R // 2) : (way + 1) * (R // 2)].astype(BF)
+                src, dst = zs1.at[h, way, :, cols], zr1.at[h, way, :, cols]
+                send(src, dst, z1s.at[0], z1r.at[h], ctx, (z + STEP[way]) % N)
 
         mixed_for(h, 2, store)
-        for way in (RIGHT, LEFT):
-            send(zs1.at[h, way], zr1.at[h, way], z1s.at[h], z1r.at[h], ctx, (z + STEP[way]) % N)
 
     def mix_send(h, way, part):
         src, dst = zs2.at[h, way, part], zr2.at[h, way, part]
-        send(src, dst, z2s.at[h], z2r.at[h], ctx, (z + STEP[way]) % N)
+        send(src, dst, z2s.at[0], z2r.at[h], ctx, (z + STEP[way]) % N)
 
     def mix_plain(h, way):
         part = 1 - way
@@ -486,17 +486,17 @@
     gather_relay(C2)
     finish(C1)
     spread(C1)
+    gather_rest(C2, RIGHT)
+    project(C2, 3)
     spread_relay_q(C0)
     spread_relay_kv(C0)
-    gather_rest(C2, RIGHT)
-    project(C2, 3)
     gather_rest(C2, LEFT)
     project(C2, 1)
     gather_last(C2)
+    spread_relay_q(C1)
+    spread_relay_kv(C1)
     project(C2, 2)
     finish(C2)
-    spread_relay_q(C1)
-    spread_relay_kv(C1)
     spread(C2)
     spread_sibling_q(C0)
     spread_sibling_q(C1)
@@ -506,16 +506,18 @@
     spread_rest_kv(C1)
     attend([(EARLY, rel, True) for rel in near], early[:3])
     spread_sibling_q(C2)
+    attend([(LATE, 0, True)], early[:3])
     spread_last_q(C0)
     spread_last_q(C1)
-    attend([(EARLY, 2, True), (LATE, 0, True)], early[:3])
-    spread_relay_q(C2)
     spread_last_kv(C0)
     spread_last_kv(C1)
-    attend([(EARLY, rel, False) for rel in (1, 3, 0, 2)] + [(LATE, 0, False)], early[3:])
+    attend([(EARLY, 2, True)], early)
+    spread_relay_q(C2)
     sum_far(0)
+    attend([(EARLY, rel, False) for rel in near] + [(LATE, 0, False)], early[3:])
     spread_rest_q(C2)
-    attend([(LATE, 1, True), (LATE, 3, True)], early)
+    attend([(LATE, 1, True)], early)
+    attend([(LATE, 3, True)], early)
     spread_relay_kv(C2)
     sum_plain(0, RIGHT)
     sum_plain(0, LEFT)
@@ -548,19 +550,16 @@
     mix_last(0)
     mix_passed(1)
     mix_last(1)
-    for h, first, count, at in (C0, C1, C2):
-        rows = pl.ds(first, count)
-        left_here(xg.at[h, pl.ds(0, 3), rows], gs.at[at])
-        left_here(kv.at[h, pl.ds(0, 3), :, :, rows], xs.at[at, 0])
-        left_here(qb.at[h, pl.ds(0, 3), :, rows], xs.at[at, 1])
-        left_here(oq.at[1 - c, h, rows], xs.at[at, 2])
-        left_here(okv.at[1 - c, h, :, rows], xs.at[at, 3])
-    for h in range(2):
-        left_here(os1.at[h], o1s.at[h])
-        left_here(os2.at[h], o2s.at[h])
-        left_here(oss.at[h], oqs.at[h])
-        left_here(zs1.at[h], z1s.at[h])
-        left_here(zs2.at[h], z2s.at[h])
+    left_here(xg.at[:, pl.ds(0, 3)], gs.at[0])
+    left_here(kv.at[:, pl.ds(0, 3)], xs.at[0])
+    left_here(qb.at[:, pl.ds(0, 3)], xs.at[1])
+    left_here(oq.at[1 - c], xs.at[2])
+    left_here(okv.at[1 - c], xs.at[3])
+    left_here(os1, o1s.at[0])
+    left_here(os2, o2s.at[0])
+    left_here(oss, oqs.at[0])
+    left_here(zs1, z1s.at[0])
+    left_here(zs2, z2s.at[0])
     for copy in outgoing:
         copy.wait()
 
@@ -606,19 +605,19 @@
             pltpu.VMEM((2, 2, 2, R // 2, DW), BF),
             pltpu.VMEM((2, R, DW), BF),
             dma((9,)),
-            dma((3,)),
+            dma((1,)),
             dma((3, 4)),
-            dma((3, 4)),
+            dma((4,)),
             dma((3, 8)),
+            dma((1,)),
             dma((2,)),
+            dma((1,)),
             dma((2,)),
+            dma((1,)),
             dma((2,)),
+            dma((1,)),
             dma((2,)),
-            dma((2,)),
-            dma((2,)),
-            dma((2,)),
-            dma((2,)),
-            dma((2,)),
+            dma((1,)),
             dma((2,)),
         ],
         compiler_params=pltpu.CompilerParams(

time: 64.1 us -> 62.6 us (0.977)
  Pallas kernels: 62.2 us -> 60.7 us
    pallas_call x1, Pallas kernels: 62.2 us -> 60.7 us  [per_device(): pl.pallas_call(kernel, name='attention_layer', out_shape=jax.ShapeDtypeSt...]
where the time goes in v4:
time: 62.6 us; the launch traced here: 62.5 us
  Pallas kernels  60.7 us (97%)
  local copies, waits for them, and re-layouts  1.77 us (3%)
    pallas_call x1, Pallas kernels, per_device(): pl.pallas_call(kernel, name='attention_layer', out_shape=jax.ShapeDtypeSt...  60.7 us
    unnamed x1, local copies, waits for them, and re-layouts  1.77 us

profile of v4, /device:TPU:0, one launch (start us, length us, event | category | flops | bytes accessed | tf_op | source)
XLA Modules:
  0.0 62.5 jit_solution(13451469210476568741)
XLA Ops:
  0.0 60.7 %attention_layer.1 = bf16[256,768]{1,0:T(8,128)(2,1)} custom-call(s32[128]{0:T(128)} %perm_hbm.1, f32[384,128]{1,0:T(8,128)} %constant.2.clone.tab_hbm, bf16[256,768]{1,0:T(8,128)(2,1)} %tok.1, bf16[3,3072,768]{2,1,0:T(8,128)(2,1)} %wqkv.1, bf16[768,3072]{1,0:T(8,128)(2,1)} %wout.1), custom_call_target="tpu_custom_call" | custom-call | tf_op jit(solution)/shard_map/attention_layer/pallas_call | solution.py:571
  60.7 1.8 %copy.7 = bf16[256,768]{1,0:T(8,128)(2,1)} copy(bf16[256,768]{1,0:T(8,128)(2,1)} %attention_layer.1) | data formatting | bytes 786432

commit v5 on v4

--- a/solution.py
+++ b/solution.py
@@ -359,18 +359,22 @@
             pack(os1.at[h, way], h, far, way)
             send(os1.at[h, way], or1.at[h, way], o1s.at[0], o1r.at[h], my_q(STEP[way], c), z)
 
-    def sum_near(h, way, core, plus=None):
+    def near_pack(h, way, core, plus=None):
         pack(os2.at[h, way, core], h, (qc + STEP[way]) % N, core, plus)
-        dst = or2.at[h, c, way]
-        send(os2.at[h, way, core], dst, o2s.at[0], o2r.at[h], my_q(STEP[way], core), z)
+
+    def near_send(h, way, core):
+        src, dst = os2.at[h, way, core], or2.at[h, c, way]
+        send(src, dst, o2s.at[0], o2r.at[h], my_q(STEP[way], core), z)
 
     def sum_plain(h, way):
-        sum_near(h, way, 1 - way)
+        near_pack(h, way, 1 - way)
+        near_send(h, way, 1 - way)
 
     def sum_passed(h):
         arrive(or1.at[h], o1r.at[h])
         for way in (RIGHT, LEFT):
-            sum_near(h, way, way, or1.at[h, way])
+            near_pack(h, way, way, or1.at[h, way])
+            near_send(h, way, way)
 
     def sum_sibling(h):
         pack(oss.at[h], h, qc, 1 - c)
@@ -407,10 +411,10 @@
         def store(cols, part):
             for way in (RIGHT, LEFT):
                 zs1[h, way, :, cols] = part[way * (R // 2) : (way + 1) * (R // 2)].astype(BF)
-                src, dst = zs1.at[h, way, :, cols], zr1.at[h, way, :, cols]
-                send(src, dst, z1s.at[0], z1r.at[h], ctx, (z + STEP[way]) % N)
 
         mixed_for(h, 2, store)
+        for way in (RIGHT, LEFT):
+            send(zs1.at[h, way], zr1.at[h, way], z1s.at[0], z1r.at[h], ctx, (z + STEP[way]) % N)
 
     def mix_send(h, way, part):
         src, dst = zs2.at[h, way, part], zr2.at[h, way, part]
@@ -517,16 +521,18 @@
     attend([(EARLY, rel, False) for rel in near] + [(LATE, 0, False)], early[3:])
     spread_rest_q(C2)
     attend([(LATE, 1, True)], early)
+    spread_relay_kv(C2)
     attend([(LATE, 3, True)], early)
-    spread_relay_kv(C2)
-    sum_plain(0, RIGHT)
-    sum_plain(0, LEFT)
+    near_pack(0, RIGHT, LEFT)
+    near_pack(0, LEFT, RIGHT)
     sum_sibling(0)
     spread_rest_kv(C2)
     attend([(LATE, rel, False) for rel in near], late[:3])
-    sum_passed(0)
+    near_send(0, RIGHT, LEFT)
+    near_send(0, LEFT, RIGHT)
     spread_last_q(C2)
     attend([(LATE, 2, True)], early + late[:3])
+    sum_passed(0)
     spread_last_kv(C2)
     attend([(LATE, 2, False)], late[3:])
     sum_far(1)
@@ -537,9 +543,9 @@
     wo_in.wait()
     normalize(0)
     mix_far(0)
+    sum_passed(1)
     mix_plain(0, RIGHT)
     mix_plain(0, LEFT)
-    sum_passed(1)
     mix_own(0)
     mix_passed(0)
     normalize(1)

time: 62.6 us -> 62.4 us (level)
  no operation moved by 1% of the time
where the time goes in v5:
time: 62.4 us; the launch traced here: 62 us
  Pallas kernels  60.3 us (97%)
  local copies, waits for them, and re-layouts  1.77 us (3%)
    pallas_call x1, Pallas kernels, per_device(): pl.pallas_call(kernel, name='attention_layer', out_shape=jax.ShapeDtypeSt...  60.3 us
    unnamed x1, local copies, waits for them, and re-layouts  1.77 us

profile of v5, /device:TPU:0, one launch (start us, length us, event | category | flops | bytes accessed | tf_op | source)
XLA Modules:
  0.0 62.0 jit_solution(13611180251078151900)
XLA Ops:
  0.0 60.3 %attention_layer.1 = bf16[256,768]{1,0:T(8,128)(2,1)} custom-call(s32[128]{0:T(128)} %perm_hbm.1, f32[384,128]{1,0:T(8,128)} %constant.2.clone.tab_hbm, bf16[256,768]{1,0:T(8,128)(2,1)} %tok.1, bf16[3,3072,768]{2,1,0:T(8,128)(2,1)} %wqkv.1, bf16[768,3072]{1,0:T(8,128)(2,1)} %wout.1), custom_call_target="tpu_custom_call" | custom-call | tf_op jit(solution)/shard_map/attention_layer/pallas_call | solution.py:577
  60.3 1.8 %copy.7 = bf16[256,768]{1,0:T(8,128)(2,1)} copy(bf16[256,768]{1,0:T(8,128)(2,1)} %attention_layer.1) | data formatting | bytes 786432

commit v6 on v5

--- a/solution.py
+++ b/solution.py
@@ -204,33 +204,49 @@
         partner = target + jnp.where(low, distance, -distance)
         swap[...] = jnp.where(source == partner, 1.0, 0.0).astype(BF)
 
-    def finish(chunk):
+    def finish(chunk, j):
         h, first, count, _ = chunk
         mine = pl.ds(first, count)
         cosine = cost[pl.ds(h * R + first, count), :]
         sine = sint[pl.ds(h * R + first, count), :]
-        for j in range(2):
-            pairs = [acc[h, mine, pl.ds(j * DW + i * 2 * HD, 2 * HD)] for i in range(HH)]
-            stacked = jnp.concatenate([p.astype(BF) for p in pairs], axis=0)
-            other = jnp.dot(stacked, swap[...], preferred_element_type=F32)
-            for head in range(2 * HH):
-                cols = slice(head % 2 * HD, (head % 2 + 1) * HD)
-                v = pairs[head // 2][:, cols]
-                w = other[head // 2 * count : (head // 2 + 1) * count, cols]
-                square = jnp.mean(v * v, axis=-1, keepdims=True)
-                factor = lax.rsqrt(square + EPSILON)
-                if j == 0:
-                    factor = factor * (HD**-0.5 / math.log(2.0))
-                turned = ((v * cosine + w * sine) * factor).astype(BF)
-                half, to = head // HH, pl.ds(head % HH * HD, HD)
-                if j == 0:
-                    oq[half, h, mine, to] = turned
-                else:
-                    okv[half, h, 0, mine, to] = turned
-        for half in range(2):
-            okv[half, h, 1, mine] = acc[h, mine, pl.ds(2 * DW + half * HW, HW)].astype(BF)
-
-    def spread(chunk):
+        if j == 2:
+            for half in range(2):
+                okv[half, h, 1, mine] = acc[h, mine, pl.ds(2 * DW + half * HW, HW)].astype(BF)
+            return
+        pairs = [acc[h, mine, pl.ds(j * DW + i * 2 * HD, 2 * HD)] for i in range(HH)]
+        stacked = jnp.concatenate([p.astype(BF) for p in pairs], axis=0)
+        other = jnp.dot(stacked, swap[...], preferred_element_type=F32)
+        for head in range(2 * HH):
+            cols = slice(head % 2 * HD, (head % 2 + 1) * HD)
+            v = pairs[head // 2][:, cols]
+            w = other[head // 2 * count : (head // 2 + 1) * count, cols]
+            square = jnp.mean(v * v, axis=-1, keepdims=True)
+            factor = lax.rsqrt(square + EPSILON)
+            if j == 0:
+                factor = factor * (HD**-0.5 / math.log(2.0))
+            turned = ((v * cosine + w * sine) * factor).astype(BF)
+            half, to = head // HH, pl.ds(head % HH * HD, HD)
+            if j == 0:
+                oq[half, h, mine, to] = turned
+            else:
+                okv[half, h, 0, mine, to] = turned
+
+    def project_last(chunk):
+        h, first, count, _ = chunk
+        src = (z + 2) % N
+        rows = pl.ds(pl.multiple_of(src * DW, DW), DW)
+        mine = pl.ds(first, count)
+        for j in range(3):
+            acc[h, mine, pl.ds(j * DW, DW)] += jnp.dot(
+                xg[h, src, mine], wq[j, rows, :], preferred_element_type=F32
+            )
+            finish(chunk, j)
+            if j == 0:
+                spread_q(chunk)
+            else:
+                spread_kv(chunk, j - 1)
+
+    def spread_q(chunk):
         h, first, count, at = chunk
         rows = pl.ds(first, count)
         for turn in range(2):
@@ -244,18 +260,21 @@
             oq.at[1 - c, h, rows], qb.at[h, kc, c, rows], xs.at[2], xr.at[at, 2], sibling, z
         )
         qb[h, qc, c, rows] = oq[c, h, rows]
-        for turn in range(2):
-            for half in range(2):
-                kslot = (x, y)[half]
-                for way in (RIGHT, LEFT):
-                    part = way ^ turn
-                    src, dst = okv.at[half, h, part, rows], kv.at[h, kslot, c, part, rows]
-                    send(src, dst, xs.at[0], xr.at[at, 4 + turn], kv_to(half, STEP[way]), z)
-        send(
-            okv.at[1 - c, h, :, rows], kv.at[h, qc, c, :, rows],
-            xs.at[3], xr.at[at, 6], sibling, z,
-        )
-        kv[h, kc, c, :, rows] = okv[c, h, :, rows]
+
+    def spread_kv(chunk, part):
+        h, first, count, at = chunk
+        rows = pl.ds(first, count)
+        for half in range(2):
+            kslot = (x, y)[half]
+            for way in (RIGHT, LEFT):
+                src, dst = okv.at[half, h, part, rows], kv.at[h, kslot, c, part, rows]
+                send(src, dst, xs.at[0], xr.at[at, 4 + part], kv_to(half, STEP[way]), z)
+        if part == 1:
+            send(
+                okv.at[1 - c, h, :, rows], kv.at[h, qc, c, :, rows],
+                xs.at[3], xr.at[at, 6], sibling, z,
+            )
+            kv[h, kc, c, :, rows] = okv[c, h, :, rows]
 
     def spread_relay_q(chunk):
         h, first, count, at = chunk
@@ -265,13 +284,13 @@
                 block = qb.at[h, (qc + N - STEP[way]) % N, core, halves(chunk)[way]]
                 send(block, block, xs.at[1], xr.at[at, 3], my_q(STEP[way], c), z)
 
-    def spread_relay_kv(chunk):
-        h, first, count, at = chunk
-        arrive(kv.at[h, kc, :, :, pl.ds(first, count)], xr.at[at, 4])
-        for way in (RIGHT, LEFT):
-            for core in range(2):
-                block = kv.at[h, (kc + N - STEP[way]) % N, core, way, pl.ds(first, count)]
-                send(block, block, xs.at[1], xr.at[at, 7], my_kv(STEP[way]), z)
+    def spread_relay_kv(chunk, part):
+        h, first, count, at = chunk
+        rows = pl.ds(first, count)
+        arrive(kv.at[h, kc, :, :, rows], xr.at[at, 4 + part])
+        for way in (RIGHT, LEFT):
+            block = kv.at[h, (kc + N - STEP[way]) % N, way, part, rows]
+            send(block, block, xs.at[1], xr.at[at, 7], my_kv(STEP[way]), z)
 
     def spread_sibling_q(chunk):
         h, first, count, at = chunk
@@ -284,7 +303,6 @@
     def spread_rest_kv(chunk):
         h, first, count, at = chunk
         arrive(kv.at[h, kc, 1 - c, :, pl.ds(first, count)], xr.at[at, 6])
-        arrive(kv.at[h, kc, :, :, pl.ds(first, count)], xr.at[at, 5])
 
     def spread_last_q(chunk):
         h, first, count, at = chunk
@@ -478,30 +496,26 @@
     project(C0, 1)
     weights(3)
     gather_last(C0)
-    project(C0, 2)
-    finish(C0)
-    spread(C0)
+    project_last(C0)
     gather_rest(C1, RIGHT)
     project(C1, 3)
     gather_rest(C1, LEFT)
     project(C1, 1)
     gather_last(C1)
-    project(C1, 2)
+    project_last(C1)
     gather_relay(C2)
-    finish(C1)
-    spread(C1)
     gather_rest(C2, RIGHT)
     project(C2, 3)
     spread_relay_q(C0)
-    spread_relay_kv(C0)
+    spread_relay_kv(C0, 0)
     gather_rest(C2, LEFT)
     project(C2, 1)
+    spread_relay_kv(C0, 1)
     gather_last(C2)
     spread_relay_q(C1)
-    spread_relay_kv(C1)
-    project(C2, 2)
-    finish(C2)
-    spread(C2)
+    spread_relay_kv(C1, 0)
+    project_last(C2)
+    spread_relay_kv(C1, 1)
     spread_sibling_q(C0)
     spread_sibling_q(C1)
     spread_rest_q(C0)
@@ -521,12 +535,13 @@
     attend([(EARLY, rel, False) for rel in near] + [(LATE, 0, False)], early[3:])
     spread_rest_q(C2)
     attend([(LATE, 1, True)], early)
-    spread_relay_kv(C2)
+    spread_relay_kv(C2, 0)
     attend([(LATE, 3, True)], early)
     near_pack(0, RIGHT, LEFT)
     near_pack(0, LEFT, RIGHT)
     sum_sibling(0)
     spread_rest_kv(C2)
+    spread_relay_kv(C2, 1)
     attend([(LATE, rel, False) for rel in near], late[:3])
     near_send(0, RIGHT, LEFT)
     near_send(0, LEFT, RIGHT)

time: 62.4 us -> 67.3 us (1.079)
  Pallas kernels: 60.3 us -> 65.3 us
    pallas_call x1, Pallas kernels: 60.3 us -> 65.3 us  [per_device(): pl.pallas_call(kernel, name='attention_layer', out_shape=jax.ShapeDtypeSt...]
where the time goes in v6:
time: 67.3 us; the launch traced here: 67.1 us
  Pallas kernels  65.3 us (97%)
  local copies, waits for them, and re-layouts  1.77 us (3%)
    pallas_call x1, Pallas kernels, per_device(): pl.pallas_call(kernel, name='attention_layer', out_shape=jax.ShapeDtypeSt...  65.3 us
    unnamed x1, local copies, waits for them, and re-layouts  1.77 us

profile of v6, /device:TPU:0, one launch (start us, length us, event | category | flops | bytes accessed | tf_op | source)
XLA Modules:
  0.0 67.1 jit_solution(18289203414055839115)
XLA Ops:
  0.0 65.3 %attention_layer.1 = bf16[256,768]{1,0:T(8,128)(2,1)} custom-call(s32[128]{0:T(128)} %perm_hbm.1, f32[384,128]{1,0:T(8,128)} %constant.2.clone.tab_hbm, bf16[256,768]{1,0:T(8,128)(2,1)} %tok.1, bf16[3,3072,768]{2,1,0:T(8,128)(2,1)} %wqkv.1, bf16[768,3072]{1,0:T(8,128)(2,1)} %wout.1), custom_call_target="tpu_custom_call" | custom-call | tf_op jit(solution)/shard_map/attention_layer/pallas_call | solution.py:592
  65.4 1.8 %copy.7 = bf16[256,768]{1,0:T(8,128)(2,1)} copy(bf16[256,768]{1,0:T(8,128)(2,1)} %attention_layer.1) | data formatting | bytes 786432
